TPU v7x, 128 devices: a whole 4x4x4 slice. The times are simulated.
128 devices in a mesh: tm: 16 (over y, x), batch: 8 (over z, core).
Axes of the slice: x: 4, y: 4, z: 4, core: 2. Of those that a mesh axis runs over, the one named last changes fastest.
Arguments:
- obs_feats: bfloat16 [32, 1024, 2048], P('batch', 'tm'), may hold values from -6 to 6
- next_feats: bfloat16 [32, 1024, 2048], P('batch', 'tm'), may hold values from -6 to 6
- online_w: float32 [2048, 2048], P(('tm', 'batch')), may hold values from -6 to 6
- target_w: float32 [2048, 2048], P(('tm', 'batch')), may hold values from -6 to 6
- log_decay: float32 [2048], replicated, may hold values from -1 to 0, as said below
- step_scale: float32 [32, 1024], P('batch', 'tm'), may hold values from 0.5 to 2
- online_heads: float32 [2, 2048], replicated, may hold values from -6 to 6
- target_heads: float32 [2, 2048], replicated, may hold values from -6 to 6
- reward: float32 [32, 1024], P('batch', 'tm'), may hold values from -6 to 6
- next_action_log_prob: float32 [32, 1024], P('batch', 'tm'), may hold values from -3 to 1
- resets: int32 [32, 1024], P('batch', 'tm'), may hold values 0 or 1
- horizon: int32 [32], P('batch'), may hold values from 1 to 8
- burn_in: int32 [32], P('batch'), may hold values from 0 to 64
Outputs:
- grad_w: float32 [2048, 2048], P(('tm', 'batch'))
- new_target: float32 [2048, 2048], P(('tm', 'batch'))
- returns: float32 [32, 1024], P('batch', 'tm')
Inputs may be any that keep to these rules, and one draw needn't show every extreme that they name: `log_decay`: every entry is negative.
All inputs are finite; a program needn't handle non-finite values. No bound on the sum of `resets` on one device may be relied on, other than what follows from the above.
Results may differ from a plain program's by a relative error of at most 0.0059.
Values may be sent and summed in bfloat16 or wider, within the bound.
A program may use at most 128 MiB of HBM per device.

v0:
```python
import jax
import jax.numpy as jnp
from jax import lax
from jax.experimental import pallas as pl
from jax.experimental.pallas import tpu as pltpu
from jax.sharding import PartitionSpec as P

NMAX = 8
DISCOUNT = 0.99
ENTROPY_COEFF = 0.2
POLYAK_RATE = 0.005
STEP_SIZE = 0.1

F32 = jnp.float32
BF16 = jnp.bfloat16
MESH = pl.DeviceIdType.MESH

D = 2048
H = 2048
HALF = H // 2
T = 64
PAIR = 8
ROWS = T * PAIR
TM = 16
SCALE = D ** (-0.5)

WIDTHS = (384, 384, 256)
OFFSETS = (0, 384, 768)
ORDERS = (("z", "x", "y"), ("y", "z", "x"), ("x", "y", "z"))
HALVED = ((None, "z", "x"), (None, "y", "y"), (None, "x", "y"))
AG_MESSAGES = 6


def half_shape(k, w):
    return ((16, w), (2, 32, w), (2, 4, 32, w))[k]


def kernel(
    obs, nxt, onw, tgw, ld, step, onh, tgh, rew, logp, rst, hor, burn,
    gw, nt, ret,
    xr_o, xr_n, xp_o, xp_n, xt, wst,
    wt0, wt1, wt2, wo0, wo1, wo2,
    pk_m, pk_i, bc0, bc1, cc, ss, pf, tp, vt, vo,
    sf, dall, ends_t, ends_o, lv, carry,
    q_s, q_r, nb_s, nb_r, du,
    g0, g1, g2,
    s00, s01, s02, s10, s11, s12, s20, s21, s22,
    r00, r01, r02, r10, r11, r12, r20, r21, r22,
    gx_s, gx_r,
    ag_ss, ag_rs, rs_ss, rs_rs, pre_ss, pre_rs, loc_sem, d2d_ss, d2d_rs, nb_sem,
):
    tm = lax.axis_index("tm")
    batch = lax.axis_index("batch")
    y, x = tm // 4, tm % 4
    z, c = batch // 2, batch % 2
    at = {"y": y, "x": x, "z": z}
    other = 1 - c
    wb = ((wt0, wt1, wt2), (wo0, wo1, wo2))
    gg = (g0, g1, g2)
    snd = ((s00, s01, s02), (s10, s11, s12), (s20, s21, s22))
    rcv = ((r00, r01, r02), (r10, r11, r12), (r20, r21, r22))
    pending = []

    def device(**moved):
        here = {**at, **moved}
        return {"tm": here["y"] * 4 + here["x"], "batch": here["z"] * 2 + c}

    partner = {"tm": tm, "batch": z * 2 + other}

    def remote(src, dst, ss_, rs_, dev):
        return pltpu.make_async_remote_copy(
            src_ref=src, dst_ref=dst, send_sem=ss_, recv_sem=rs_, device_id=dev,
            device_id_type=MESH,
        )

    def send(src, dst, ss_, rs_, dev):
        copy = remote(src, dst, ss_, rs_, dev)
        copy.start()
        pending.append(copy)

    mine = pl.ds(pl.multiple_of(c * HALF, HALF), HALF)
    theirs = pl.ds(pl.multiple_of(other * HALF, HALF), HALF)
    own_rows = pl.ds(pl.multiple_of(c * 16, 16), 16)
    for m, w in enumerate((tgw, onw)):
        wst[m] = w[:, theirs].astype(BF16)
        for p in range(3):
            cols = pl.ds(pl.multiple_of(c * HALF + OFFSETS[p], 128), WIDTHS[p])
            wb[m][p][y, x, z, own_rows, :] = w[:, cols].astype(BF16)

    row8 = lax.broadcasted_iota(jnp.int32, (PAIR, 128), 0)
    lane8 = lax.broadcasted_iota(jnp.int32, (PAIR, 128), 1)
    row_own = (row8[:, :T] // 4) == c

    def twice(v):
        return jnp.where(row_own, jnp.concatenate([v, v], axis=0), 0.0)

    pk_m[...] = jnp.zeros_like(pk_m)
    for slot, r in enumerate((step, rew, logp)):
        pk_m[slot, :, :T] = twice(r[...])
    pk_m[3, :, :T] = twice(rst[...].astype(F32))
    hz = jnp.zeros((PAIR, 128), F32)
    bz = jnp.zeros((PAIR, 128), F32)
    for i in range(4):
        sel = row8 == c * 4 + i
        hz = jnp.where(sel, hor[i].astype(F32), hz)
        bz = jnp.where(sel, burn[i].astype(F32), bz)
    pk_m[4] = hz
    pk_m[5] = bz

    own_half = pl.ds(pl.multiple_of(c * 256, 256), 256)
    local = [
        pltpu.make_async_copy(nxt, xr_n.at[own_half, :], loc_sem.at[0]),
        pltpu.make_async_copy(obs, xr_o.at[own_half, :], loc_sem.at[1]),
    ]
    for copy in local:
        copy.start()

    barrier = pltpu.get_barrier_semaphore()
    peers = [partner, device(z=lax.rem(z + 1, 4)), device(z=lax.rem(z + 3, 4))]
    peers += [{"tm": lax.rem(tm + d, TM), "batch": batch} for d in range(1, TM)]
    for dev in peers:
        pl.semaphore_signal(barrier, inc=1, device_id=dev, device_id_type=MESH)
    pl.semaphore_wait(barrier, len(peers))

    def w_half(m, p):
        cols = pl.ds(OFFSETS[p], WIDTHS[p])
        return wst.at[m, :, cols], wb[m][p].at[y, x, z, own_rows, :]

    def w_half_in(m, p):
        rows = pl.ds(pl.multiple_of(other * 16, 16), 16)
        dst = wb[m][p].at[y, x, z, rows, :]
        remote(dst, dst, d2d_ss.at[m * 3 + p], d2d_rs.at[m * 3 + p], partner).wait_recv()

    for m in range(2):
        for p in range(3):
            src, dst = w_half(m, p)
            send(src, dst, d2d_ss.at[m * 3 + p], d2d_rs.at[m * 3 + p], partner)
    send(pk_m, pk_i, d2d_ss.at[6], d2d_rs.at[6], partner)
    send(nxt, xr_n.at[own_half, :], d2d_ss.at[7], d2d_rs.at[7], partner)
    send(obs, xr_o.at[own_half, :], d2d_ss.at[8], d2d_rs.at[8], partner)

    def block(p, k, q, h):
        order = ORDERS[p]
        idx = {}
        for a in "yxz":
            if a in order[:k]:
                idx[a] = pl.ds(0, 4)
            elif a == order[k]:
                idx[a] = q
            else:
                idx[a] = at[a]
        rows = pl.ds(0, 32)
        if h is not None:
            if k == 0:
                rows = pl.ds(16 * h, 16)
            else:
                idx[HALVED[p][k]] = pl.ds(2 * h, 2)
        return (idx["y"], idx["x"], idx["z"], rows, pl.ds(0, WIDTHS[p]))

    def around(p, k):
        axis = ORDERS[p][k]
        q = at[axis]
        return (
            axis, q, lax.rem(q + 1, 4), lax.rem(q + 3, 4), lax.rem(q + 2, 4),
            device(**{axis: lax.rem(q + 1, 4)}), device(**{axis: lax.rem(q + 3, 4)}),
        )

    def ag_sem(m, p, k, j):
        n = ((m * 3 + p) * 3 + k) * AG_MESSAGES + j
        return ag_ss.at[n], ag_rs.at[n]

    def ag_send(m, p, k, q, h, j, dev):
        ref = wb[m][p].at[block(p, k, q, h)]
        send(ref, ref, *ag_sem(m, p, k, j), dev)

    def ag_wait(m, p, k, q, h, j, dev):
        ref = wb[m][p].at[block(p, k, q, h)]
        remote(ref, ref, *ag_sem(m, p, k, j), dev).wait_recv()

    def ag_first(m, p, k):
        _, q, _, _, _, plus, minus = around(p, k)
        if k == 2:
            ag_send(m, p, k, q, 0, 0, plus)
            ag_send(m, p, k, q, 1, 2, minus)
            ag_send(m, p, k, q, 1, 1, plus)
            ag_send(m, p, k, q, 0, 3, minus)
        else:
            ag_send(m, p, k, q, None, 0, plus)
            ag_send(m, p, k, q, None, 2, minus)

    def ag_forward(m, p, k):
        _, q, qp, qm, _, plus, minus = around(p, k)
        h0, h1 = (0, 1) if k == 2 else (None, None)
        ag_wait(m, p, k, qm, h0, 0, minus)
        ag_send(m, p, k, qm, 0, 4, plus)
        ag_wait(m, p, k, qp, h1, 2, plus)
        ag_send(m, p, k, qp, 1, 5, minus)

    def ag_last(m, p, k):
        _, q, qp, qm, opp, plus, minus = around(p, k)
        if k == 2:
            ag_wait(m, p, k, qm, 1, 1, minus)
            ag_wait(m, p, k, qp, 0, 3, plus)
        ag_wait(m, p, k, opp, 0, 4, minus)
        ag_wait(m, p, k, opp, 1, 5, plus)

    for m in range(2):
        for p in range(3):
            w_half_in(m, p)
            ag_first(m, p, 0)
    for m in range(2):
        for p in range(3):
            ag_forward(m, p, 0)
    for m in range(2):
        for p in range(3):
            ag_last(m, p, 0)
            ag_first(m, p, 1)
    for m in range(2):
        for p in range(3):
            ag_forward(m, p, 1)
    for p in range(3):
        ag_last(0, p, 1)
        ag_first(0, p, 2)

    remote(pk_m, pk_i, d2d_ss.at[6], d2d_rs.at[6], partner).wait_recv()
    step8 = pk_m[0] + pk_i[0]
    rew8 = pk_m[1] + pk_i[1]
    logp8 = pk_m[2] + pk_i[2]
    rst8 = pk_m[3] + pk_i[3]
    keep8 = 1.0 - rst8
    hor8 = pk_m[4] + pk_i[4]
    burn8 = pk_m[5] + pk_i[5]

    sf[tm, 0] = jnp.broadcast_to(jnp.sum(step8, axis=1, keepdims=True), (PAIR, 128))
    sf[tm, 1] = jnp.broadcast_to(1.0 - jnp.max(rst8, axis=1, keepdims=True), (PAIR, 128))
    for d in range(1, TM):
        dev = {"tm": lax.rem(tm + d, TM), "batch": batch}
        send(sf.at[tm], sf.at[tm], pre_ss.at[0, d], pre_rs.at[0, tm], dev)

    def spread_lanes(dst, v):
        for t in range(T):
            dst[pl.ds(t * PAIR, PAIR), :] = jnp.broadcast_to(v[:, t : t + 1], (PAIR, 128))

    spread_lanes(bc0, step8)
    spread_lanes(bc1, keep8)
    ld8 = jnp.broadcast_to(ld[:, mine], (PAIR, HALF))

    def wide(v):
        return jnp.concatenate([v] * (HALF // 128), axis=1)

    def at_t(t):
        return pl.ds(pl.multiple_of(t * PAIR, PAIR), PAIR)

    def factors(t, prod):
        e = jnp.exp(wide(bc0[at_t(t), :]) * ld8)
        f = e * wide(bc1[at_t(t), :])
        cc[at_t(t), :] = f
        ss[at_t(t), :] = jnp.sqrt(1.0 - e * e)
        prod = prod * f
        pf[at_t(t), :] = prod
        return prod

    lax.fori_loop(0, T, factors, jnp.ones((PAIR, HALF), F32))

    def tails(i, prod):
        t = T - 1 - i
        tp[at_t(t), :] = prod
        return prod * cc[at_t(t), :]

    lax.fori_loop(0, T, tails, jnp.ones((PAIR, HALF), F32))

    r_out = lax.broadcasted_iota(jnp.int32, (ROWS, ROWS), 0)
    r_in = lax.broadcasted_iota(jnp.int32, (ROWS, ROWS), 1)

    def permutation():
        return jnp.where(r_out == (r_in % T) * PAIR + r_in // T, 1.0, 0.0).astype(BF16)

    for p in range(3):
        ag_forward(0, p, 2)
    for p in range(3):
        ag_last(1, p, 1)
        ag_first(1, p, 2)

    other_half = pl.ds(pl.multiple_of(other * 256, 256), 256)
    local[0].wait()
    remote(nxt, xr_n.at[other_half, :], d2d_ss.at[7], d2d_rs.at[7], partner).wait_recv()
    local[1].wait()
    remote(obs, xr_o.at[other_half, :], d2d_ss.at[8], d2d_rs.at[8], partner).wait_recv()
    perm = permutation()

    def permute(i, _):
        cols = pl.ds(pl.multiple_of(i * 256, 256), 256)
        xp_n[:, cols] = jnp.dot(perm, xr_n[:, cols], preferred_element_type=F32).astype(BF16)
        v = jnp.dot(perm, xr_o[:, cols], preferred_element_type=F32)
        xp_o[:, cols] = v.astype(BF16)
        xt[cols, :] = v.T.astype(BF16)
        return 0

    lax.fori_loop(0, D // 256, permute, 0)

    for d in range(1, TM):
        j = lax.rem(tm + d, TM)
        dev = {"tm": j, "batch": batch}
        remote(sf.at[j], sf.at[j], pre_ss.at[0, d], pre_rs.at[0, j], dev).wait_recv()

    def block_decay(j, _):
        dall[j] = jnp.exp(wide(sf[j, 0]) * ld8) * wide(sf[j, 1])
        return 0

    lax.fori_loop(0, TM, block_decay, 0)

    def project(m, p, xp, v):
        def tile(i, _):
            rows = pl.ds(pl.multiple_of(i * 256, 256), 256)
            w = wb[m][p][...].reshape(D, WIDTHS[p])
            acc = jnp.dot(xp[rows, :], w, preferred_element_type=F32)
            v[rows, pl.ds(OFFSETS[p], WIDTHS[p])] = acc * SCALE
            return 0

        lax.fori_loop(0, ROWS // 256, tile, 0)

    def scan(v):
        def body(t, st):
            st = cc[at_t(t), :] * st + ss[at_t(t), :] * v[at_t(t), :]
            v[at_t(t), :] = st
            return st

        return lax.fori_loop(0, T, body, jnp.zeros((PAIR, HALF), F32))

    def prefix_send(n, ends, forward):
        for d in range(TM - 1, 0, -1):
            to = tm + d if forward else tm - d

            @pl.when(to < TM if forward else to >= 0)
            def _(d=d, to=to):
                dev = {"tm": to, "batch": batch}
                remote(ends.at[tm], ends.at[tm], pre_ss.at[n, d], pre_rs.at[n, tm], dev).start()

    def prefix_take(n, ends, forward):
        carry[...] = jnp.zeros_like(carry)
        for j in range(TM) if forward else range(TM - 1, -1, -1):

            @pl.when(j < tm if forward else j > tm)
            def _(j=j):
                dev = {"tm": j, "batch": batch}
                remote(ends.at[j], ends.at[j], pre_ss.at[n, 0], pre_rs.at[n, j], dev).wait_recv()
                carry[...] = dall[j] * carry[...] + ends[j]

    def prefix_drain(n, ends, forward):
        for d in range(1, TM):
            to = tm + d if forward else tm - d

            @pl.when(to < TM if forward else to >= 0)
            def _(d=d, to=to):
                dev = {"tm": to, "batch": batch}
                remote(ends.at[tm], ends.at[tm], pre_ss.at[n, d], pre_rs.at[n, tm], dev).wait_send()

    def lane_fold(v):
        out = v[:, :128]
        for i in range(1, HALF // 128):
            out = out + v[:, i * 128 : (i + 1) * 128]
        return jnp.sum(out, axis=1, keepdims=True)

    def quality(v, heads, slot):
        h0 = jnp.broadcast_to(heads[0:1, mine], (PAIR, HALF))
        h1 = jnp.broadcast_to(heads[1:2, mine], (PAIR, HALF))
        start = carry[...]

        def body(t, acc):
            st = v[at_t(t), :] + pf[at_t(t), :] * start
            v[at_t(t), :] = st
            act = st / (1.0 + jnp.exp(-st))
            here = lane8 == t
            return (
                jnp.where(here, lane_fold(act * h0), acc[0]),
                jnp.where(here, lane_fold(act * h1), acc[1]),
            )

        zero = jnp.zeros((PAIR, 128), F32)
        a0, a1 = lax.fori_loop(0, T, body, (zero, zero))
        q_s[slot, 0] = a0
        q_s[slot, 1] = a1
        send(q_s.at[slot], q_r.at[slot], d2d_ss.at[9 + slot], d2d_rs.at[9 + slot], partner)

    def quality_sum(slot):
        remote(
            q_s.at[slot], q_r.at[slot], d2d_ss.at[9 + slot], d2d_rs.at[9 + slot], partner
        ).wait_recv()
        return [(q_s[slot, k] + q_r[slot, k]) * (H ** (-0.5)) for k in range(2)]

    for p in range(3):
        ag_last(0, p, 2)
        project(0, p, xp_n, vt)
    for p in range(3):
        ag_forward(1, p, 2)
    ends_t[tm] = scan(vt)
    prefix_send(1, ends_t, True)
    prefix_take(1, ends_t, True)
    quality(vt, tgh, 0)
    tq = quality_sum(0)
    value8 = jnp.minimum(tq[0], tq[1]) - ENTROPY_COEFF * logp8

    nb_s[0] = rew8
    nb_s[1] = value8
    nb_s[2] = keep8
    before = {"tm": lax.rem(tm + TM - 1, TM), "batch": batch}
    send(nb_s, nb_r, nb_sem.at[0], nb_sem.at[1], before)
    remote(nb_s, nb_r, nb_sem.at[0], nb_sem.at[1], before).wait_recv()
    inside = (lane8 >= T) & (lane8 < T + NMAX) & (tm < TM - 1)

    def extended(own, slot):
        later = jnp.where(inside, pltpu.roll(nb_r[slot], T, 1), 0.0)
        return jnp.where(lane8 < T, own, later)

    ext_r, ext_v, ext_k = extended(rew8, 0), extended(value8, 1), extended(keep8, 2)

    def shifted(v, n):
        return v if n == 0 else pltpu.roll(v, 128 - n, 1)

    total = jnp.zeros((PAIR, 128), F32)
    alive = jnp.ones((PAIR, 128), F32)
    for n in range(NMAX):
        total = total + jnp.where(hor8 > n, DISCOUNT**n * alive * shifted(ext_r, n), 0.0)
        alive = alive * shifted(ext_k, n + 1)
        total = total + jnp.where(
            hor8 == n + 1, DISCOUNT ** (n + 1) * alive * shifted(ext_v, n + 1), 0.0
        )
    ret[...] = jnp.where(c == 0, total[:4, :T], total[4:, :T])
    weight = jnp.where((lane8 + tm * T).astype(F32) >= burn8, 1.0, 0.0)

    for p in range(3):
        ag_last(1, p, 2)
        project(1, p, xp_o, vo)
    ends_o[tm] = scan(vo)
    prefix_send(2, ends_o, True)
    prefix_take(2, ends_o, True)
    quality(vo, onh, 1)

    def slopes(t, _):
        v = vo[at_t(t), :]
        sig = 1.0 / (1.0 + jnp.exp(-v))
        vo[at_t(t), :] = sig * (1.0 + v * (1.0 - sig)) * (H ** (-0.5))
        return 0

    lax.fori_loop(0, T, slopes, 0)
    oq = quality_sum(1)
    spread_lanes(bc0, weight * (oq[0] - total))
    spread_lanes(bc1, weight * (oq[1] - total))
    h0 = jnp.broadcast_to(onh[0:1, mine], (PAIR, HALF))
    h1 = jnp.broadcast_to(onh[1:2, mine], (PAIR, HALF))

    def back(i, adj):
        t = T - 1 - i
        dh = (wide(bc0[at_t(t), :]) * h0 + wide(bc1[at_t(t), :]) * h1) * vo[at_t(t), :]
        adj = dh + adj
        vo[at_t(t), :] = adj
        return cc[at_t(t), :] * adj

    lv[tm] = lax.fori_loop(0, T, back, jnp.zeros((PAIR, HALF), F32))
    prefix_send(3, lv, False)
    prefix_take(3, lv, False)
    incoming = carry[...]
    both = jnp.concatenate([incoming, incoming], axis=0)

    def finish(i, _):
        rows = pl.ds(pl.multiple_of(i * 16, 16), 16)
        adj = vo[rows, :] + tp[rows, :] * both
        du[rows, :] = (ss[rows, :] * adj).astype(BF16)
        return 0

    lax.fori_loop(0, ROWS // 16, finish, 0)

    def gradient(p):
        def tile(i, _):
            rows = pl.ds(pl.multiple_of(i * 512, 512), 512)
            v = jnp.dot(
                xt[rows, :], du[:, pl.ds(OFFSETS[p], WIDTHS[p])], preferred_element_type=F32
            )
            gg[p][i] = (v * SCALE).reshape(4, 4, 32, WIDTHS[p])
            return 0

        lax.fori_loop(0, 4, tile, 0)

    def pieces(p, k, q, h, fn):
        order = ORDERS[p]
        if k == 0:
            fn(block(p, k, q, h), ())
            return
        free = [a for a in "yxz" if a in order[:k]]

        def at_piece(ids):
            idx = dict(at)
            idx[order[k]] = q
            for a, i in zip(free, ids):
                idx[a] = i + 2 * h if a == HALVED[p][k] else i
            return (idx["y"], idx["x"], idx["z"], pl.ds(0, 32), pl.ds(0, WIDTHS[p]))

        if k == 1:
            for i in range(2):
                fn(at_piece((i,)), (i,))
            return

        def body(n, _):
            i, j = n // 4, n % 4
            fn(at_piece((i, j)), (i, j))
            return 0

        lax.fori_loop(0, 8, body, 0)

    def rs_sem(p, k, j):
        n = (p * 3 + k) * 6 + j
        return rs_ss.at[n], rs_rs.at[n]

    def rs_send(p, k, j, dev):
        send(snd[p][k].at[j], rcv[p][k].at[j], *rs_sem(p, k, j), dev)

    def rs_wait(p, k, j):
        _, _, _, _, _, plus, minus = around(p, k)
        dev = plus if j % 2 == 0 else minus
        remote(snd[p][k].at[j], rcv[p][k].at[j], *rs_sem(p, k, j), dev).wait_recv()

    def rs_fill(p, k, j, q, h, add):
        def fn(idx, at_):
            v = gg[p][idx]
            if add:
                v = v + rcv[p][k][(j - 4,) + at_].astype(F32)
            snd[p][k][(j,) + at_] = v.astype(BF16)

        pieces(p, k, q, h, fn)

    def rs_first(p, k):
        _, q, qp, qm, opp, plus, minus = around(p, k)
        for j, (who, h, dev) in enumerate(
            ((opp, 0, minus), (opp, 1, plus), (qm, 1, minus), (qp, 0, plus))
        ):
            rs_fill(p, k, j, who, h, False)
            rs_send(p, k, j, dev)

    def rs_middle(p, k):
        _, q, qp, qm, opp, plus, minus = around(p, k)
        for j, (who, h, dev) in ((4, (qm, 0, minus)), (5, (qp, 1, plus))):
            rs_wait(p, k, j - 4)
            rs_fill(p, k, j, who, h, True)
            rs_send(p, k, j, dev)

    def rs_last(p, k):
        q = at[ORDERS[p][k]]
        for h, pair in ((0, (3, 4)), (1, (2, 5))):
            for j in pair:
                rs_wait(p, k, j)

            def fn(idx, at_, pair=pair):
                v = gg[p][idx]
                for j in pair:
                    v = v + rcv[p][k][(j,) + at_].astype(F32)
                gg[p][idx] = v

            pieces(p, k, q, h, fn)

    for p in range(3):
        gradient(p)
        rs_first(p, 2)
    for p in range(3):
        rs_middle(p, 2)
    for k in (1, 0):
        for p in range(3):
            rs_last(p, k + 1)
            rs_first(p, k)
        for p in range(3):
            rs_middle(p, k)
    for p in range(3):
        rs_last(p, 0)

    other_rows = pl.ds(pl.multiple_of(other * 16, 16), 16)
    for p in range(3):
        gx_s[:, pl.ds(OFFSETS[p], WIDTHS[p])] = gg[p][y, x, z, other_rows, :]
    send(gx_s, gx_r, d2d_ss.at[11], d2d_rs.at[11], partner)
    for p in range(3):
        cols = pl.ds(pl.multiple_of(c * HALF + OFFSETS[p], 128), WIDTHS[p])
        gw[:, cols] = gg[p][y, x, z, own_rows, :]
    remote(gx_s, gx_r, d2d_ss.at[11], d2d_rs.at[11], partner).wait_recv()
    gw[:, theirs] = gx_r[...]
    nt[...] = (1.0 - POLYAK_RATE) * tgw[...] + POLYAK_RATE * (onw[...] - STEP_SIZE * gw[...])

    prefix_drain(1, ends_t, True)
    prefix_drain(2, ends_o, True)
    prefix_drain(3, lv, False)
    for copy in pending:
        copy.wait_send()


def shards(
    obs_feats, next_feats, online_w, target_w, log_decay, step_scale, online_heads, target_heads,
    reward, next_action_log_prob, resets, horizon, burn_in,
):
    vmem = pl.BlockSpec(memory_space=pltpu.VMEM)
    smem = pl.BlockSpec(memory_space=pltpu.SMEM)
    hbm = pl.BlockSpec(memory_space=pl.ANY)
    weights = [pltpu.VMEM((4, 4, 4, 32, w), BF16) for w in WIDTHS]
    staged = [pltpu.VMEM((6, *half_shape(k, w)), BF16) for w in WIDTHS for k in range(3)]
    big = pltpu.VMEM((ROWS, HALF), F32)
    ends = pltpu.VMEM((TM, PAIR, HALF), F32)
    narrow = pltpu.VMEM((ROWS, 128), F32)
    scratch = [
        pltpu.VMEM((ROWS, D), BF16), pltpu.VMEM((ROWS, D), BF16),
        pltpu.VMEM((ROWS, D), BF16), pltpu.VMEM((ROWS, D), BF16),
        pltpu.VMEM((D, ROWS), BF16), pltpu.VMEM((2, 16, HALF), BF16),
        *weights, *weights,
        pltpu.VMEM((6, PAIR, 128), F32), pltpu.VMEM((6, PAIR, 128), F32), narrow, narrow,
        big, big, big, big, big, big,
        pltpu.VMEM((TM, 2, PAIR, 128), F32), ends, ends, ends, ends,
        pltpu.VMEM((PAIR, HALF), F32),
        pltpu.VMEM((2, 2, PAIR, 128), F32), pltpu.VMEM((2, 2, PAIR, 128), F32),
        pltpu.VMEM((3, PAIR, 128), F32), pltpu.VMEM((3, PAIR, 128), F32),
        pltpu.VMEM((ROWS, HALF), BF16),
        *[pltpu.VMEM((4, 4, 4, 32, w), F32) for w in WIDTHS],
        *staged, *staged,
        pltpu.VMEM((16, HALF), F32), pltpu.VMEM((16, HALF), F32),
        pltpu.SemaphoreType.DMA((18 * AG_MESSAGES,)), pltpu.SemaphoreType.DMA((18 * AG_MESSAGES,)),
        pltpu.SemaphoreType.DMA((54,)), pltpu.SemaphoreType.DMA((54,)),
        pltpu.SemaphoreType.DMA((4, TM)), pltpu.SemaphoreType.DMA((4, TM)),
        pltpu.SemaphoreType.DMA((2,)),
        pltpu.SemaphoreType.DMA((12,)), pltpu.SemaphoreType.DMA((12,)),
        pltpu.SemaphoreType.DMA((2,)),
    ]
    rows_b, span, width = obs_feats.shape
    return pl.pallas_call(
        kernel,
        name="critic_step",
        out_shape=(
            jax.ShapeDtypeStruct(online_w.shape, F32),
            jax.ShapeDtypeStruct(target_w.shape, F32),
            jax.ShapeDtypeStruct(reward.shape, F32),
        ),
        in_specs=[hbm, hbm] + [vmem] * 9 + [smem] * 2,
        out_specs=(vmem, vmem, vmem),
        scratch_shapes=scratch,
        compiler_params=pltpu.CompilerParams(
            collective_id=0, has_side_effects=True, vmem_limit_bytes=62 * 1024 * 1024
        ),
    )(
        obs_feats.reshape(rows_b * span, width), next_feats.reshape(rows_b * span, width),
        online_w, target_w, log_decay[None], step_scale, online_heads, target_heads,
        reward, next_action_log_prob, resets, horizon, burn_in,
    )


def solution(mesh):
    return jax.shard_map(
        shards,
        mesh=mesh,
        in_specs=(
            P("batch", "tm", None), P("batch", "tm", None),
            P(("tm", "batch"), None), P(("tm", "batch"), None),
            P(), P("batch", "tm"), P(), P(),
            P("batch", "tm"), P("batch", "tm"), P("batch", "tm"), P("batch"), P("batch"),
        ),
        out_specs=(P(("tm", "batch"), None), P(("tm", "batch"), None), P("batch", "tm")),
        check_vma=False,
    )
```

profile of v0, /device:TPU:1, one launch (start us, length us, event | category | flops | bytes accessed | tf_op | source)
XLA Modules:
  0.0 145.6 jit_solution(17787926435523111625)
XLA Ops:
  0.6 142.1 %critic_step.1 = (f32[16,2048]{1,0:T(8,128)}, f32[16,2048]{1,0:T(8,128)}, f32[4,64]{1,0:T(4,128)}) custom-call(bf16[256,2048]{1,0:T(8,128)(2,1)} %bitcast.3, bf16[256,2048]{1,0:T(8,128)(2,1)} %bitcast.4, f32[16,2048]{1,0:T(8,128)} %onw.1, f32[16,2048]{1,0:T(8,128)} %tgw.1, f32[1,2048]{1,0:T(1,128)} %bitcast.5, f32[4,64]{1,0:T(4,128)} %step.1, ...), custom_call_target="tpu_custom_call" | custom-call | tf_op jit(solution)/shard_map/critic_step/pallas_call | solution.py:627
  142.7 0.0 copy-start
  142.7 1.6 %copy.19 = f32[16,2048]{1,0:T(8,128)} copy(f32[16,2048]{1,0:T(8,128)} %get-tuple-element.6) | data formatting | bytes 262144
  144.3 0.0 copy-done
  144.4 0.0 copy-start.1
  144.4 0.7 copy.20
  145.0 0.0 copy-done.1
  145.0 0.6 copy.21
Async XLA Ops:
  142.7 1.6 %copy-start = (f32[16,2048]{1,0:T(8,128)S(1)}, f32[16,2048]{1,0:T(8,128)}, u32[]{:S(2)}) copy-start(f32[16,2048]{1,0:T(8,128)} %get-tuple-element.7) | copy-start | bytes 393220
  144.4 0.7 copy-start.1
where the time goes:
time: 146 us
  Pallas kernels  142 us (97%)
  local copies, waits for them, and re-layouts  2.86 us (2%)
    pallas_call x1, Pallas kernels, shards(): pl.pallas_call(kernel, name='critic_step', out_shape=(jax.ShapeDtypeStruc...  142 us

commit v1 on v0

v1 whole, which is shorter than its diff:
```python
import jax
import jax.numpy as jnp
from jax import lax
from jax.experimental import pallas as pl
from jax.experimental.pallas import tpu as pltpu
from jax.sharding import PartitionSpec as P

NMAX = 8
DISCOUNT = 0.99
ENTROPY_COEFF = 0.2
POLYAK_RATE = 0.005
STEP_SIZE = 0.1

F32 = jnp.float32
BF16 = jnp.bfloat16
MESH = pl.DeviceIdType.MESH

D = 2048
H = 2048
HALF = H // 2
T = 64
PAIR = 8
ROWS = T * PAIR
TM = 16
SCALE = D ** (-0.5)

WIDTHS = (384, 384, 256)
OFFSETS = (0, 384, 768)
ORDERS = (("z", "x", "y"), ("y", "z", "x"), ("x", "y", "z"))
PARTS = (2, 0, 1)
AG_SEMS = 23
RS_SEMS = 23
LINES = (2, 3, 1, 0)


def kernel(
    obs, nxt, onw, tgw, ld, step, onh, tgh, rew, logp, rst, hor, burn,
    gw, ret,
    xr_o, xr_n, xp_o, xp_n, xt, wst,
    wt0, wt1, wt2, wo0, wo1, wo2,
    pk_m, pk_i, bc0, bc1, qa0, qa1, cc, ss, pf, tp, vt, vo,
    sf, dall, ends_t, ends_o, lv, carry,
    q_s, q_r, nb_s, nb_r, du,
    g0, g1, g2,
    sh0, sh1, sh2, sw0, sw1, sw2, sb0, sb1, sb2,
    rh0, rh1, rh2, rw0, rw1, rw2, rb0, rb1, rb2,
    gx_s, gx_r,
    ag_ss, ag_rs, rs_ss, rs_rs, pre_ss, pre_rs, loc_sem, d2d_ss, d2d_rs, nb_sem,
):
    tm = lax.axis_index("tm")
    batch = lax.axis_index("batch")
    y, x = tm // 4, tm % 4
    z, c = batch // 2, batch % 2
    at = {"y": y, "x": x, "z": z}
    other = 1 - c
    wb = ((wt0, wt1, wt2), (wo0, wo1, wo2))
    gg = (g0, g1, g2)
    snd_h, snd_w, snd_b = (sh0, sh1, sh2), (sw0, sw1, sw2), (sb0, sb1, sb2)
    rcv_h, rcv_w, rcv_b = (rh0, rh1, rh2), (rw0, rw1, rw2), (rb0, rb1, rb2)
    pending = []

    def device(**moved):
        here = {**at, **moved}
        return {"tm": here["y"] * 4 + here["x"], "batch": here["z"] * 2 + c}

    partner = {"tm": tm, "batch": z * 2 + other}

    def remote(src, dst, ss_, rs_, dev):
        return pltpu.make_async_remote_copy(
            src_ref=src, dst_ref=dst, send_sem=ss_, recv_sem=rs_, device_id=dev,
            device_id_type=MESH,
        )

    def send(src, dst, ss_, rs_, dev):
        copy = remote(src, dst, ss_, rs_, dev)
        copy.start()
        pending.append(copy)

    mine = pl.ds(pl.multiple_of(c * HALF, HALF), HALF)
    theirs = pl.ds(pl.multiple_of(other * HALF, HALF), HALF)
    own_rows = pl.ds(pl.multiple_of(c * 16, 16), 16)
    other_rows = pl.ds(pl.multiple_of(other * 16, 16), 16)
    for m, w in enumerate((tgw, onw)):
        wst[m] = w[:, theirs].astype(BF16)
        for p in range(3):
            cols = pl.ds(pl.multiple_of(c * HALF + OFFSETS[p], 128), WIDTHS[p])
            wb[m][p][y, x, z, own_rows, :] = w[:, cols].astype(BF16)

    row8 = lax.broadcasted_iota(jnp.int32, (PAIR, 128), 0)
    lane8 = lax.broadcasted_iota(jnp.int32, (PAIR, 128), 1)
    row_own = (row8[:, :T] // 4) == c

    def twice(v):
        return jnp.where(row_own, jnp.concatenate([v, v], axis=0), 0.0)

    pk_m[...] = jnp.zeros_like(pk_m)
    for slot, r in enumerate((step, rew, logp)):
        pk_m[slot, :, :T] = twice(r[...])
    pk_m[3, :, :T] = twice(rst[...].astype(F32))
    hz = jnp.zeros((PAIR, 128), F32)
    bz = jnp.zeros((PAIR, 128), F32)
    for i in range(4):
        sel = row8 == c * 4 + i
        hz = jnp.where(sel, hor[i].astype(F32), hz)
        bz = jnp.where(sel, burn[i].astype(F32), bz)
    pk_m[4] = hz
    pk_m[5] = bz

    own_half = pl.ds(pl.multiple_of(c * 256, 256), 256)
    other_half = pl.ds(pl.multiple_of(other * 256, 256), 256)
    local = [
        pltpu.make_async_copy(nxt, xr_n.at[own_half, :], loc_sem.at[0]),
        pltpu.make_async_copy(obs, xr_o.at[own_half, :], loc_sem.at[1]),
    ]
    for copy in local:
        copy.start()

    barrier = pltpu.get_barrier_semaphore()
    peers = [partner] + [device(z=lax.rem(z + d, 4)) for d in range(1, 4)]
    peers += [{"tm": lax.rem(tm + d, TM), "batch": batch} for d in range(1, TM)]
    for dev in peers:
        pl.semaphore_signal(barrier, inc=1, device_id=dev, device_id_type=MESH)
    pl.semaphore_wait(barrier, len(peers))

    def w_half(m, p):
        cols = pl.ds(OFFSETS[p], WIDTHS[p])
        return wst.at[m, :, cols], wb[m][p].at[y, x, z, own_rows, :]

    def w_half_in(m, p):
        dst = wb[m][p].at[y, x, z, other_rows, :]
        remote(dst, dst, d2d_ss.at[m * 3 + p], d2d_rs.at[m * 3 + p], partner).wait_recv()

    for m in range(2):
        for p in range(3):
            src, dst = w_half(m, p)
            send(src, dst, d2d_ss.at[m * 3 + p], d2d_rs.at[m * 3 + p], partner)
    send(pk_m, pk_i, d2d_ss.at[6], d2d_rs.at[6], partner)
    send(nxt, xr_n.at[own_half, :], d2d_ss.at[7], d2d_rs.at[7], partner)
    send(obs, xr_o.at[own_half, :], d2d_ss.at[8], d2d_rs.at[8], partner)

    def place(p, first, second, last):
        idx = dict(zip(ORDERS[p], (first, second, last)))
        return idx["y"], idx["x"], idx["z"]

    def turned(p, i, d):
        return lax.rem(at[ORDERS[p][i]] + d, 4)

    def toward(p, i, d):
        return device(**{ORDERS[p][i]: turned(p, i, d)})

    FULL = pl.ds(0, 4)

    def half_of(h):
        return FULL if h is None else pl.ds(2 * h, 2)

    def ag_copy(m, p, j, where, dev):
        ref = wb[m][p].at[where]
        n = (m * 3 + p) * AG_SEMS + j
        return remote(ref, ref, ag_ss.at[n], ag_rs.at[n], dev)

    def ag_send(m, p, j, where, dev):
        copy = ag_copy(m, p, j, where, dev)
        copy.start()
        pending.append(copy)

    def ag_wait(m, p, j, where, dev):
        ag_copy(m, p, j, where, dev).wait_recv()

    def line(p, second, last, h=None):
        return place(p, half_of(h), second, last)

    def ag_one(m, p):
        for d in (2, 1, 3):
            ag_send(m, p, d - 1, (y, x, z), toward(p, 0, d))

    def ag_one_in(m, p):
        for d in (1, 3, 2):
            where = place(p, turned(p, 0, 4 - d), turned(p, 1, 0), turned(p, 2, 0))
            ag_wait(m, p, d - 1, where, toward(p, 0, 4 - d))

    def ag_two(m, p):
        own = line(p, turned(p, 1, 0), turned(p, 2, 0))
        ag_send(m, p, 3, own, toward(p, 1, 1))
        ag_send(m, p, 4, own, toward(p, 1, 3))

    def ag_two_forward(m, p):
        q3 = turned(p, 2, 0)
        ag_wait(m, p, 3, line(p, turned(p, 1, 3), q3), toward(p, 1, 3))
        ag_send(m, p, 5, line(p, turned(p, 1, 3), q3, 0), toward(p, 1, 1))
        ag_wait(m, p, 4, line(p, turned(p, 1, 1), q3), toward(p, 1, 1))
        ag_send(m, p, 6, line(p, turned(p, 1, 1), q3, 1), toward(p, 1, 3))

    def ag_two_last(m, p):
        q3 = turned(p, 2, 0)
        ag_wait(m, p, 5, line(p, turned(p, 1, 2), q3, 0), toward(p, 1, 3))
        ag_wait(m, p, 6, line(p, turned(p, 1, 2), q3, 1), toward(p, 1, 1))

    def ag_three(m, p, l):
        own = line(p, turned(p, 1, l), turned(p, 2, 0))
        ag_send(m, p, 7 + 4 * l, own, toward(p, 2, 1))
        ag_send(m, p, 8 + 4 * l, own, toward(p, 2, 3))

    def ag_three_forward(m, p, l):
        second = turned(p, 1, l)
        ag_wait(m, p, 7 + 4 * l, line(p, second, turned(p, 2, 3)), toward(p, 2, 3))
        ag_send(m, p, 9 + 4 * l, line(p, second, turned(p, 2, 3), 0), toward(p, 2, 1))
        ag_wait(m, p, 8 + 4 * l, line(p, second, turned(p, 2, 1)), toward(p, 2, 1))
        ag_send(m, p, 10 + 4 * l, line(p, second, turned(p, 2, 1), 1), toward(p, 2, 3))

    def ag_three_last(m, p):
        for l in range(4):
            second = turned(p, 1, l)
            ag_wait(m, p, 9 + 4 * l, line(p, second, turned(p, 2, 2), 0), toward(p, 2, 3))
            ag_wait(m, p, 10 + 4 * l, line(p, second, turned(p, 2, 2), 1), toward(p, 2, 1))

    def cols_of(p):
        return pl.ds(OFFSETS[p], WIDTHS[p])

    def wide(v, w=HALF):
        return jnp.concatenate([v] * (w // 128), axis=1)

    def at_t(t):
        return pl.ds(pl.multiple_of(t * PAIR, PAIR), PAIR)

    def spread_lanes(dst, v):
        for t in range(T):
            dst[pl.ds(t * PAIR, PAIR), :] = jnp.broadcast_to(v[:, t : t + 1], (PAIR, 128))

    r_out = lax.broadcasted_iota(jnp.int32, (ROWS, ROWS), 0)
    r_in = lax.broadcasted_iota(jnp.int32, (ROWS, ROWS), 1)

    def permutation():
        return jnp.where(r_out == (r_in % T) * PAIR + r_in // T, 1.0, 0.0).astype(BF16)

    def permute_next():
        perm = permutation()

        def body(i, _):
            cols = pl.ds(pl.multiple_of(i * 256, 256), 256)
            xp_n[:, cols] = jnp.dot(perm, xr_n[:, cols], preferred_element_type=F32).astype(BF16)
            return 0

        lax.fori_loop(0, D // 256, body, 0)

    def permute_obs(lo, hi):
        perm = permutation()

        def body(i, _):
            cols = pl.ds(pl.multiple_of(i * 256, 256), 256)
            v = jnp.dot(perm, xr_o[:, cols], preferred_element_type=F32)
            xp_o[:, cols] = v.astype(BF16)
            xt[i // 2, pl.ds(2 * (i % 2), 2)] = v.T.astype(BF16).reshape(2, 4, 32, ROWS)
            return 0

        lax.fori_loop(lo, hi, body, 0)

    def project(m, p, xp, v):
        def tile(i, _):
            rows = pl.ds(pl.multiple_of(i * 256, 256), 256)
            w = wb[m][p][...].reshape(D, WIDTHS[p])
            acc = jnp.dot(xp[rows, :], w, preferred_element_type=F32)
            v[rows, cols_of(p)] = acc * SCALE
            return 0

        lax.fori_loop(0, ROWS // 256, tile, 0)

    def scan(v, p, ends):
        cols = cols_of(p)

        def body(i, st):
            for k in range(4):
                rows = at_t(i * 4 + k)
                st = cc[rows, cols] * st + ss[rows, cols] * v[rows, cols]
                v[rows, cols] = st
            return st

        ends[tm, :, cols] = lax.fori_loop(0, T // 4, body, jnp.zeros((PAIR, WIDTHS[p]), F32))

    def ends_copy(n, ends, p, slot, d, dev):
        cols = pl.ds(0, HALF) if p is None else cols_of(p)
        ref = ends.at[slot, :, cols]
        return remote(ref, ref, pre_ss.at[n, d], pre_rs.at[n, slot], dev)

    def prefix_send(n, ends, p, forward):
        for d in range(TM - 1, 0, -1):
            to = tm + d if forward else tm - d

            @pl.when(to < TM if forward else to >= 0)
            def _(d=d, to=to):
                ends_copy(n, ends, p, tm, d, {"tm": to, "batch": batch}).start()

    def prefix_take(n, ends, p, forward):
        cols = pl.ds(0, HALF) if p is None else cols_of(p)
        carry[:, cols] = jnp.zeros_like(carry[:, cols])
        for j in range(TM - 1) if forward else range(TM - 1, 0, -1):

            @pl.when(j < tm if forward else j > tm)
            def _(j=j):
                ends_copy(n, ends, p, j, 0, {"tm": j, "batch": batch}).wait_recv()
                carry[:, cols] = dall[j, :, cols] * carry[:, cols] + ends[j, :, cols]

    def prefix_drain(n, ends, p, forward):
        for d in range(1, TM):
            to = tm + d if forward else tm - d

            @pl.when(to < TM if forward else to >= 0)
            def _(d=d, to=to):
                ends_copy(n, ends, p, tm, d, {"tm": to, "batch": batch}).wait_send()

    def quality(v, heads, p, fresh, slope):
        cols, w = cols_of(p), WIDTHS[p]
        hcols = pl.ds(pl.multiple_of(c * HALF + OFFSETS[p], 128), w)
        h0 = jnp.broadcast_to(heads[0:1, hcols], (PAIR, w))
        h1 = jnp.broadcast_to(heads[1:2, hcols], (PAIR, w))
        start = carry[:, cols]

        def fold(u):
            out = u[:, :128]
            for i in range(1, w // 128):
                out = out + u[:, i * 128 : (i + 1) * 128]
            return out

        def body(i, _):
            for k in range(4):
                rows = at_t(i * 4 + k)
                st = v[rows, cols] + pf[rows, cols] * start
                sig = 1.0 / (1.0 + jnp.exp(-st))
                act = st * sig
                if slope:
                    v[rows, cols] = (sig + act * (1.0 - sig)) * (H ** (-0.5))
                f0, f1 = fold(act * h0), fold(act * h1)
                qa0[rows, :] = f0 if fresh else qa0[rows, :] + f0
                qa1[rows, :] = f1 if fresh else qa1[rows, :] + f1
            return 0

        lax.fori_loop(0, T // 4, body, 0)

    def quality_send(slot):
        def body(i, acc):
            a0, a1 = acc
            for k in range(8):
                rows = at_t(i * 8 + k)
                here = lane8 == i * 8 + k
                a0 = jnp.where(here, jnp.sum(qa0[rows, :], axis=1, keepdims=True), a0)
                a1 = jnp.where(here, jnp.sum(qa1[rows, :], axis=1, keepdims=True), a1)
            return a0, a1

        zero = jnp.zeros((PAIR, 128), F32)
        a0, a1 = lax.fori_loop(0, T // 8, body, (zero, zero))
        q_s[slot, 0] = a0
        q_s[slot, 1] = a1
        send(q_s.at[slot], q_r.at[slot], d2d_ss.at[9 + slot], d2d_rs.at[9 + slot], partner)

    def quality_sum(slot):
        remote(
            q_s.at[slot], q_r.at[slot], d2d_ss.at[9 + slot], d2d_rs.at[9 + slot], partner
        ).wait_recv()
        return [(q_s[slot, k] + q_r[slot, k]) * (H ** (-0.5)) for k in range(2)]

    for m in range(2):
        for p in range(3):
            w_half_in(m, p)
            ag_one(m, p)
    for p in range(3):
        ag_one_in(0, p)
        ag_two(0, p)
        ag_three(0, p, 0)
    for p in range(3):
        ag_one_in(1, p)
        ag_two(1, p)
    remote(pk_m, pk_i, d2d_ss.at[6], d2d_rs.at[6], partner).wait_recv()
    step8 = pk_m[0] + pk_i[0]
    rew8 = pk_m[1] + pk_i[1]
    logp8 = pk_m[2] + pk_i[2]
    rst8 = pk_m[3] + pk_i[3]
    keep8 = 1.0 - rst8
    hor8 = pk_m[4] + pk_i[4]
    burn8 = pk_m[5] + pk_i[5]

    sf[tm, 0] = jnp.broadcast_to(jnp.sum(step8, axis=1, keepdims=True), (PAIR, 128))
    sf[tm, 1] = jnp.broadcast_to(1.0 - jnp.max(rst8, axis=1, keepdims=True), (PAIR, 128))
    for d in range(1, TM):
        dev = {"tm": lax.rem(tm + d, TM), "batch": batch}
        send(sf.at[tm], sf.at[tm], pre_ss.at[0, d], pre_rs.at[0, tm], dev)

    spread_lanes(bc0, step8)
    spread_lanes(bc1, keep8)
    ld8 = jnp.broadcast_to(ld[:, mine], (PAIR, HALF))

    def factors(t, prod):
        e = jnp.exp(wide(bc0[at_t(t), :]) * ld8)
        f = e * wide(bc1[at_t(t), :])
        cc[at_t(t), :] = f
        ss[at_t(t), :] = jnp.sqrt(1.0 - e * e)
        prod = prod * f
        pf[at_t(t), :] = prod
        return prod

    lax.fori_loop(0, T, factors, jnp.ones((PAIR, HALF), F32))
    for p in range(3):
        ag_two_forward(0, p)
        ag_three(0, p, 3)
        ag_three(0, p, 1)
    for p in range(3):
        ag_three_forward(0, p, 0)
    local[0].wait()
    remote(nxt, xr_n.at[other_half, :], d2d_ss.at[7], d2d_rs.at[7], partner).wait_recv()
    permute_next()
    for p in range(3):
        ag_two_forward(1, p)
        ag_three(1, p, 0)
    for p in range(3):
        ag_two_last(0, p)
        ag_three(0, p, 2)
    def tails(i, prod):
        t = T - 1 - i
        tp[at_t(t), :] = prod
        return prod * cc[at_t(t), :]

    lax.fori_loop(0, T, tails, jnp.ones((PAIR, HALF), F32))
    local[1].wait()
    remote(obs, xr_o.at[other_half, :], d2d_ss.at[8], d2d_rs.at[8], partner).wait_recv()
    for l in (3, 1):
        for p in range(3):
            ag_three_forward(0, p, l)
    for p in range(3):
        ag_three(1, p, 3)
        ag_three(1, p, 1)
        ag_two_last(1, p)
    permute_obs(0, 4)
    for p in range(3):
        ag_three_forward(0, p, 2)
        ag_three(1, p, 2)
    permute_obs(4, 8)

    for d in range(1, TM):
        j = lax.rem(tm + d, TM)
        dev = {"tm": j, "batch": batch}
        remote(sf.at[j], sf.at[j], pre_ss.at[0, d], pre_rs.at[0, j], dev).wait_recv()

    def block_decay(j, _):
        dall[j] = jnp.exp(wide(sf[j, 0]) * ld8) * wide(sf[j, 1])
        return 0

    lax.fori_loop(0, TM, block_decay, 0)

    for p in range(3):
        ag_three_forward(1, p, 0)
    for p in PARTS[:2]:
        ag_three_last(0, p)
        project(0, p, xp_n, vt)
        scan(vt, p, ends_t)
    for p in range(3):
        ag_three_forward(1, p, 3)
    for p in PARTS[2:]:
        ag_three_last(0, p)
        project(0, p, xp_n, vt)
        scan(vt, p, ends_t)
    prefix_send(1, ends_t, None, True)
    for l in (1, 2):
        for p in range(3):
            ag_three_forward(1, p, l)
    ag_three_last(1, PARTS[0])
    project(1, PARTS[0], xp_o, vo)
    scan(vo, PARTS[0], ends_o)
    prefix_send(2 + PARTS[0], ends_o, PARTS[0], True)
    prefix_take(1, ends_t, None, True)
    for p in PARTS:
        quality(vt, tgh, p, p == PARTS[0], False)
    quality_send(0)
    for p in PARTS[1:]:
        ag_three_last(1, p)
    for p in PARTS[1:]:
        project(1, p, xp_o, vo)
        scan(vo, p, ends_o)
        prefix_send(2 + p, ends_o, p, True)
    tq = quality_sum(0)
    value8 = jnp.minimum(tq[0], tq[1]) - ENTROPY_COEFF * logp8
    nb_s[0] = rew8
    nb_s[1] = value8
    nb_s[2] = keep8
    before = {"tm": lax.rem(tm + TM - 1, TM), "batch": batch}
    send(nb_s, nb_r, nb_sem.at[0], nb_sem.at[1], before)
    prefix_take(2 + PARTS[0], ends_o, PARTS[0], True)
    quality(vo, onh, PARTS[0], True, True)

    remote(nb_s, nb_r, nb_sem.at[0], nb_sem.at[1], before).wait_recv()
    inside = (lane8 >= T) & (lane8 < T + NMAX) & (tm < TM - 1)

    def extended(own, slot):
        later = jnp.where(inside, pltpu.roll(nb_r[slot], T, 1), 0.0)
        return jnp.where(lane8 < T, own, later)

    ext_r, ext_v, ext_k = extended(rew8, 0), extended(value8, 1), extended(keep8, 2)

    def shifted(v, n):
        return v if n == 0 else pltpu.roll(v, 128 - n, 1)

    total = jnp.zeros((PAIR, 128), F32)
    alive = jnp.ones((PAIR, 128), F32)
    for n in range(NMAX):
        total = total + jnp.where(hor8 > n, DISCOUNT**n * alive * shifted(ext_r, n), 0.0)
        alive = alive * shifted(ext_k, n + 1)
        total = total + jnp.where(
            hor8 == n + 1, DISCOUNT ** (n + 1) * alive * shifted(ext_v, n + 1), 0.0
        )
    ret[...] = jnp.where(c == 0, total[:4, :T], total[4:, :T])
    weight = jnp.where((lane8 + tm * T).astype(F32) >= burn8, 1.0, 0.0)

    for p in PARTS[1:]:
        prefix_take(2 + p, ends_o, p, True)
        quality(vo, onh, p, False, True)
    quality_send(1)
    oq = quality_sum(1)
    spread_lanes(bc0, weight * (oq[0] - total))
    spread_lanes(bc1, weight * (oq[1] - total))

    for p in PARTS:
        cols, w = cols_of(p), WIDTHS[p]
        hcols = pl.ds(pl.multiple_of(c * HALF + OFFSETS[p], 128), w)
        h0 = jnp.broadcast_to(onh[0:1, hcols], (PAIR, w))
        h1 = jnp.broadcast_to(onh[1:2, hcols], (PAIR, w))

        def back(i, adj, cols=cols, w=w, h0=h0, h1=h1):
            for k in range(4):
                rows = at_t(T - 1 - (i * 4 + k))
                dh = wide(bc0[rows, :], w) * h0 + wide(bc1[rows, :], w) * h1
                adj = dh * vo[rows, cols] + adj
                vo[rows, cols] = adj
                adj = cc[rows, cols] * adj
            return adj

        lv[tm, :, cols] = lax.fori_loop(0, T // 4, back, jnp.zeros((PAIR, w), F32))
        prefix_send(5 + p, lv, p, False)

    def finish(p):
        prefix_take(5 + p, lv, p, False)
        cols = cols_of(p)
        incoming = carry[:, cols]
        both = jnp.concatenate([incoming, incoming], axis=0)

        def body(i, _):
            for k in range(2):
                rows = pl.ds(pl.multiple_of(i * 32 + k * 16, 16), 16)
                adj = vo[rows, cols] + tp[rows, cols] * both
                du[rows, cols] = (ss[rows, cols] * adj).astype(BF16)
            return 0

        lax.fori_loop(0, ROWS // 32, body, 0)

    def gradient(p, l):
        where = place(p, FULL, turned(p, 1, l), FULL)
        lhs = xt[where].reshape(512, ROWS)
        v = jnp.dot(lhs, du[:, cols_of(p)], preferred_element_type=F32)
        gg[p][where] = v.reshape(4, 4, 32, WIDTHS[p])

    def rs_copy(p, j, src, dst, dev):
        n = p * RS_SEMS + j
        return remote(src, dst, rs_ss.at[n], rs_rs.at[n], dev)

    def rs_send(p, j, src, dst, dev):
        copy = rs_copy(p, j, src, dst, dev)
        copy.start()
        pending.append(copy)

    def rs_ref(p, s, d, h=None):
        if s < 4:
            return line(p, turned(p, 1, s), turned(p, 2, d), h)
        return line(p, turned(p, 1, d), turned(p, 2, 0), h)

    def rs_axis(s):
        return 2 if s < 4 else 1

    def rs_opposite(p, s):
        for h, d in ((0, 3), (1, 1)):
            snd_h[p][s, h] = gg[p][rs_ref(p, s, 2, h)].astype(BF16)
            rs_send(
                p, 4 * s + h, snd_h[p].at[s, h], rcv_h[p].at[s, h], toward(p, rs_axis(s), d)
            )

    def rs_neighbour(p, s, h):
        d = (3, 1)[h]
        rs_copy(
            p, 4 * s + h, snd_h[p].at[s, h], rcv_h[p].at[s, h], toward(p, rs_axis(s), 4 - d)
        ).wait_recv()
        with_recv = gg[p][rs_ref(p, s, d, h)] + rcv_h[p][s, h].astype(F32)
        snd_w[p][s, h, pl.ds(2 * h, 2)] = with_recv.astype(BF16)
        snd_w[p][s, h, pl.ds(2 - 2 * h, 2)] = gg[p][rs_ref(p, s, d, 1 - h)].astype(BF16)
        rs_send(
            p, 4 * s + 2 + h, snd_w[p].at[s, h], rcv_w[p].at[s, h], toward(p, rs_axis(s), d)
        )

    def rs_sum(p, s):
        for h, d in ((0, 1), (1, 3)):
            rs_copy(
                p, 4 * s + 2 + h, snd_w[p].at[s, h], rcv_w[p].at[s, h], toward(p, rs_axis(s), d)
            ).wait_recv()
        own = rs_ref(p, s, 0)
        both = rcv_w[p][s, 0].astype(F32) + rcv_w[p][s, 1].astype(F32)
        gg[p][own] = gg[p][own] + both

    def rs_one(p):
        for d in (2, 1, 3):
            block = gg[p][place(p, turned(p, 0, d), turned(p, 1, 0), turned(p, 2, 0))]
            snd_b[p][d - 1] = block.astype(BF16)
            rs_send(p, 19 + d, snd_b[p].at[d - 1], rcv_b[p].at[d - 1], toward(p, 0, d))

    def rs_one_sum(p):
        v = gg[p][y, x, z]
        for d in (1, 3, 2):
            rs_copy(
                p, 19 + d, snd_b[p].at[d - 1], rcv_b[p].at[d - 1], toward(p, 0, 4 - d)
            ).wait_recv()
            v = v + rcv_b[p][d - 1].astype(F32)
        gg[p][y, x, z] = v * SCALE

    for p in PARTS:
        finish(p)
        gradient(p, LINES[0])
        rs_opposite(p, LINES[0])
    for p in PARTS:
        gradient(p, LINES[1])
        rs_opposite(p, LINES[1])
    for i in range(4):
        if i < 2:
            for p in PARTS:
                gradient(p, LINES[i + 2])
                rs_opposite(p, LINES[i + 2])
        for p in PARTS:
            rs_neighbour(p, LINES[i], 0)
            rs_neighbour(p, LINES[i], 1)
    for p in PARTS:
        rs_sum(p, LINES[0])
        rs_opposite(p, 4)
    for p in PARTS:
        rs_sum(p, LINES[1])
        rs_neighbour(p, 4, 0)
        rs_sum(p, LINES[2])
        rs_neighbour(p, 4, 1)
    for p in PARTS:
        rs_sum(p, LINES[3])
    for p in PARTS:
        rs_sum(p, 4)
        rs_one(p)
    for p in PARTS:
        rs_one_sum(p)

    for p in range(3):
        gx_s[:, cols_of(p)] = gg[p][y, x, z, other_rows, :]
    send(gx_s, gx_r, d2d_ss.at[11], d2d_rs.at[11], partner)
    for p in range(3):
        cols = pl.ds(pl.multiple_of(c * HALF + OFFSETS[p], 128), WIDTHS[p])
        gw[:, cols] = gg[p][y, x, z, own_rows, :]
    remote(gx_s, gx_r, d2d_ss.at[11], d2d_rs.at[11], partner).wait_recv()
    gw[:, theirs] = gx_r[...]

    prefix_drain(1, ends_t, None, True)
    for p in range(3):
        prefix_drain(2 + p, ends_o, p, True)
        prefix_drain(5 + p, lv, p, False)
    for copy in pending:
        copy.wait_send()


def shards(
    obs_feats, next_feats, online_w, target_w, log_decay, step_scale, online_heads, target_heads,
    reward, next_action_log_prob, resets, horizon, burn_in,
):
    vmem = pl.BlockSpec(memory_space=pltpu.VMEM)
    smem = pl.BlockSpec(memory_space=pltpu.SMEM)
    hbm = pl.BlockSpec(memory_space=pl.ANY)
    weights = [pltpu.VMEM((4, 4, 4, 32, w), BF16) for w in WIDTHS]
    staged = [
        *[pltpu.VMEM((5, 2, 2, 32, w), BF16) for w in WIDTHS],
        *[pltpu.VMEM((5, 2, 4, 32, w), BF16) for w in WIDTHS],
        *[pltpu.VMEM((3, 32, w), BF16) for w in WIDTHS],
    ]
    big = pltpu.VMEM((ROWS, HALF), F32)
    ends = pltpu.VMEM((TM, PAIR, HALF), F32)
    narrow = pltpu.VMEM((ROWS, 128), F32)
    scratch = [
        pltpu.VMEM((ROWS, D), BF16), pltpu.VMEM((ROWS, D), BF16),
        pltpu.VMEM((ROWS, D), BF16), pltpu.VMEM((ROWS, D), BF16),
        pltpu.VMEM((4, 4, 4, 32, ROWS), BF16), pltpu.VMEM((2, 16, HALF), BF16),
        *weights, *weights,
        pltpu.VMEM((6, PAIR, 128), F32), pltpu.VMEM((6, PAIR, 128), F32),
        narrow, narrow, narrow, narrow,
        big, big, big, big, big, big,
        pltpu.VMEM((TM, 2, PAIR, 128), F32), ends, ends, ends, ends,
        pltpu.VMEM((PAIR, HALF), F32),
        pltpu.VMEM((2, 2, PAIR, 128), F32), pltpu.VMEM((2, 2, PAIR, 128), F32),
        pltpu.VMEM((3, PAIR, 128), F32), pltpu.VMEM((3, PAIR, 128), F32),
        pltpu.VMEM((ROWS, HALF), BF16),
        *[pltpu.VMEM((4, 4, 4, 32, w), F32) for w in WIDTHS],
        *staged, *staged,
        pltpu.VMEM((16, HALF), F32), pltpu.VMEM((16, HALF), F32),
        pltpu.SemaphoreType.DMA((6 * AG_SEMS,)), pltpu.SemaphoreType.DMA((6 * AG_SEMS,)),
        pltpu.SemaphoreType.DMA((3 * RS_SEMS,)), pltpu.SemaphoreType.DMA((3 * RS_SEMS,)),
        pltpu.SemaphoreType.DMA((8, TM)), pltpu.SemaphoreType.DMA((8, TM)),
        pltpu.SemaphoreType.DMA((2,)),
        pltpu.SemaphoreType.DMA((12,)), pltpu.SemaphoreType.DMA((12,)),
        pltpu.SemaphoreType.DMA((2,)),
    ]
    rows_b, span, width = obs_feats.shape
    grad_w, returns = pl.pallas_call(
        kernel,
        name="critic_step",
        out_shape=(
            jax.ShapeDtypeStruct(online_w.shape, F32),
            jax.ShapeDtypeStruct(reward.shape, F32),
        ),
        in_specs=[hbm, hbm] + [vmem] * 9 + [smem] * 2,
        out_specs=(vmem, vmem),
        scratch_shapes=scratch,
        compiler_params=pltpu.CompilerParams(
            collective_id=0, has_side_effects=True, vmem_limit_bytes=62 * 1024 * 1024
        ),
    )(
        obs_feats.reshape(rows_b * span, width), next_feats.reshape(rows_b * span, width),
        online_w, target_w, log_decay[None], step_scale, online_heads, target_heads,
        reward, next_action_log_prob, resets, horizon, burn_in,
    )
    new_target = (1.0 - POLYAK_RATE) * target_w + POLYAK_RATE * (online_w - STEP_SIZE * grad_w)
    return grad_w, new_target, returns


def solution(mesh):
    return jax.shard_map(
        shards,
        mesh=mesh,
        in_specs=(
            P("batch", "tm", None), P("batch", "tm", None),
            P(("tm", "batch"), None), P(("tm", "batch"), None),
            P(), P("batch", "tm"), P(), P(),
            P("batch", "tm"), P("batch", "tm"), P("batch", "tm"), P("batch"), P("batch"),
        ),
        out_specs=(P(("tm", "batch"), None), P(("tm", "batch"), None), P("batch", "tm")),
        check_vma=False,
    )
```

time: 146 us -> 117 us (0.80)
  Pallas kernels: 142 us -> 113 us
  other arithmetic: 0 us -> 1.66 us
  local copies, waits for them, and re-layouts: 2.86 us -> 1.25 us
    pallas_call x1, Pallas kernels: 142 us -> 113 us  [shards(): pl.pallas_call(kernel, name='critic_step', out_shape=(jax.ShapeDtypeStruc...]
    add x0 -> x1, other arithmetic: none -> 1.66 us  [shards(): (1.0 - POLYAK_RATE) * target_w]
    unnamed x7 -> x10, local copies, waits for them, and re-layouts: 2.86 us -> 1.25 us
where the time goes in v1:
time: 117 us
  Pallas kernels  113 us (97%)
  other arithmetic  1.66 us (1%)
  local copies, waits for them, and re-layouts  1.25 us (1%)
    pallas_call x1, Pallas kernels, shards(): pl.pallas_call(kernel, name='critic_step', out_shape=(jax.ShapeDtypeStruc...  113 us

profile of v1, /device:TPU:1, one launch (start us, length us, event | category | flops | bytes accessed | tf_op | source)
XLA Modules:
  0.0 116.9 jit_solution(1853867061086753318)
XLA Ops:
  0.6 0.0 copy-start
  0.6 0.0 copy-start.1
  0.7 113.3 %critic_step.1 = (f32[16,2048]{1,0:T(8,128)}, f32[4,64]{1,0:T(4,128)}) custom-call(bf16[256,2048]{1,0:T(8,128)(2,1)} %bitcast.3, bf16[256,2048]{1,0:T(8,128)(2,1)} %bitcast.4, f32[16,2048]{1,0:T(8,128)} %onw.1, f32[16,2048]{1,0:T(8,128)} %tgw.1, f32[1,2048]{1,0:T(1,128)} %bitcast.5, f32[4,64]{1,0:T(4,128)} %step.1, f32[2,2048]{1,0:T(2,128)} %onh.1, ...), custom_call_target="tpu_custom_call" | custom-call | tf_op jit(solution)/shard_map/critic_step/pallas_call | solution.py:705
  113.9 0.0 copy-done
  114.0 0.0 copy-done.1
  114.0 0.0 copy-start.2
  114.0 1.7 %multiply_add_fusion = f32[16,2048]{1,0:T(8,128)} fusion(f32[16,2048]{1,0:T(8,128)S(1)} %copy-done, f32[16,2048]{1,0:T(8,128)} %get-tuple-element.10, f32[16,2048]{1,0:T(8,128)S(1)} %copy-done.1), kind=kLoop, calls=%fused_computation | loop fusion | flops 163840 | bytes 524288 | tf_op jit(solution)/shard_map/add | solution.py:723
  115.6 0.0 copy-done.2
  115.6 0.0 copy-start.3
  115.6 0.7 copy.18
  116.3 0.0 copy-done.3
  116.3 0.6 copy.19
Async XLA Ops:
  0.6 113.3 %copy-start = (f32[16,2048]{1,0:T(8,128)S(1)}, f32[16,2048]{1,0:T(8,128)}, u32[]{:S(2)}) copy-start(f32[16,2048]{1,0:T(8,128)} %onw.1) | copy-start | bytes 393220
  0.6 113.3 %copy-start.1 = (f32[16,2048]{1,0:T(8,128)S(1)}, f32[16,2048]{1,0:T(8,128)}, u32[]{:S(2)}) copy-start(f32[16,2048]{1,0:T(8,128)} %tgw.1) | copy-start | bytes 393220
  114.0 1.7 %copy-start.2 = (f32[16,2048]{1,0:T(8,128)S(1)}, f32[16,2048]{1,0:T(8,128)}, u32[]{:S(2)}) copy-start(f32[16,2048]{1,0:T(8,128)} %get-tuple-element.10) | copy-start | bytes 393220
  115.6 0.7 copy-start.3

commit v2 on v1

--- a/solution.py
+++ b/solution.py
@@ -28,8 +28,8 @@
 OFFSETS = (0, 384, 768)
 ORDERS = (("z", "x", "y"), ("y", "z", "x"), ("x", "y", "z"))
 PARTS = (2, 0, 1)
-AG_SEMS = 23
-RS_SEMS = 23
+AG_SEMS = 13
+RS_SEMS = 16
 LINES = (2, 3, 1, 0)
 
 
@@ -123,20 +123,21 @@
     pl.semaphore_wait(barrier, len(peers))
 
     def w_half(m, p):
-        cols = pl.ds(OFFSETS[p], WIDTHS[p])
-        return wst.at[m, :, cols], wb[m][p].at[y, x, z, own_rows, :]
-
-    def w_half_in(m, p):
-        dst = wb[m][p].at[y, x, z, other_rows, :]
-        remote(dst, dst, d2d_ss.at[m * 3 + p], d2d_rs.at[m * 3 + p], partner).wait_recv()
+        src, dst = wst.at[m, :, cols_of(p)], wb[m][p].at[y, x, z, own_rows, :]
+        return remote(src, dst, d2d_ss.at[0], d2d_rs.at[m], partner)
+
+    def w_half_in(m):
+        remote(wst.at[m], wst.at[m], d2d_ss.at[0], d2d_rs.at[m], partner).wait_recv()
+
+    def cols_of(p):
+        return pl.ds(OFFSETS[p], WIDTHS[p])
 
     for m in range(2):
         for p in range(3):
-            src, dst = w_half(m, p)
-            send(src, dst, d2d_ss.at[m * 3 + p], d2d_rs.at[m * 3 + p], partner)
-    send(pk_m, pk_i, d2d_ss.at[6], d2d_rs.at[6], partner)
-    send(nxt, xr_n.at[own_half, :], d2d_ss.at[7], d2d_rs.at[7], partner)
-    send(obs, xr_o.at[own_half, :], d2d_ss.at[8], d2d_rs.at[8], partner)
+            w_half(m, p).start()
+    send(pk_m, pk_i, d2d_ss.at[2], d2d_rs.at[2], partner)
+    send(nxt, xr_n.at[own_half, :], d2d_ss.at[3], d2d_rs.at[3], partner)
+    send(obs, xr_o.at[own_half, :], d2d_ss.at[4], d2d_rs.at[4], partner)
 
     def place(p, first, second, last):
         idx = dict(zip(ORDERS[p], (first, second, last)))
@@ -153,68 +154,60 @@
     def half_of(h):
         return FULL if h is None else pl.ds(2 * h, 2)
 
-    def ag_copy(m, p, j, where, dev):
+    def ag_copy(m, p, k, j, where, dev):
         ref = wb[m][p].at[where]
-        n = (m * 3 + p) * AG_SEMS + j
-        return remote(ref, ref, ag_ss.at[n], ag_rs.at[n], dev)
-
-    def ag_send(m, p, j, where, dev):
-        copy = ag_copy(m, p, j, where, dev)
-        copy.start()
-        pending.append(copy)
-
-    def ag_wait(m, p, j, where, dev):
-        ag_copy(m, p, j, where, dev).wait_recv()
+        n = m * 3 + p
+        return remote(ref, ref, ag_ss.at[n * 3 + k], ag_rs.at[n * AG_SEMS + j], dev)
+
+    def ag_send(m, p, k, j, where, dev):
+        ag_copy(m, p, k, j, where, dev).start()
+
+    def ag_wait(m, p, j, where):
+        ag_copy(m, p, 0, j, where, partner).wait_recv()
+
+    def ag_drain(m, p):
+        for k, where in enumerate(((0, 0, pl.ds(0, 3)), (0, pl.ds(0, 3)), (pl.ds(0, 3),))):
+            ag_copy(m, p, k, 0, where, partner).wait_send()
 
     def line(p, second, last, h=None):
         return place(p, half_of(h), second, last)
 
     def ag_one(m, p):
         for d in (2, 1, 3):
-            ag_send(m, p, d - 1, (y, x, z), toward(p, 0, d))
+            ag_send(m, p, 0, 0, (y, x, z), toward(p, 0, d))
 
     def ag_one_in(m, p):
-        for d in (1, 3, 2):
-            where = place(p, turned(p, 0, 4 - d), turned(p, 1, 0), turned(p, 2, 0))
-            ag_wait(m, p, d - 1, where, toward(p, 0, 4 - d))
+        ag_wait(m, p, 0, (0, 0, pl.ds(0, 3)))
 
     def ag_two(m, p):
         own = line(p, turned(p, 1, 0), turned(p, 2, 0))
-        ag_send(m, p, 3, own, toward(p, 1, 1))
-        ag_send(m, p, 4, own, toward(p, 1, 3))
+        ag_send(m, p, 1, 1, own, toward(p, 1, 1))
+        ag_send(m, p, 1, 2, own, toward(p, 1, 3))
 
     def ag_two_forward(m, p):
         q3 = turned(p, 2, 0)
-        ag_wait(m, p, 3, line(p, turned(p, 1, 3), q3), toward(p, 1, 3))
-        ag_send(m, p, 5, line(p, turned(p, 1, 3), q3, 0), toward(p, 1, 1))
-        ag_wait(m, p, 4, line(p, turned(p, 1, 1), q3), toward(p, 1, 1))
-        ag_send(m, p, 6, line(p, turned(p, 1, 1), q3, 1), toward(p, 1, 3))
+        ag_wait(m, p, 1, line(p, turned(p, 1, 3), q3))
+        ag_send(m, p, 1, 3, line(p, turned(p, 1, 3), q3, 0), toward(p, 1, 1))
+        ag_wait(m, p, 2, line(p, turned(p, 1, 1), q3))
+        ag_send(m, p, 1, 3, line(p, turned(p, 1, 1), q3, 1), toward(p, 1, 3))
 
     def ag_two_last(m, p):
-        q3 = turned(p, 2, 0)
-        ag_wait(m, p, 5, line(p, turned(p, 1, 2), q3, 0), toward(p, 1, 3))
-        ag_wait(m, p, 6, line(p, turned(p, 1, 2), q3, 1), toward(p, 1, 1))
+        ag_wait(m, p, 3, line(p, turned(p, 1, 2), turned(p, 2, 0)))
 
     def ag_three(m, p, l):
         own = line(p, turned(p, 1, l), turned(p, 2, 0))
-        ag_send(m, p, 7 + 4 * l, own, toward(p, 2, 1))
-        ag_send(m, p, 8 + 4 * l, own, toward(p, 2, 3))
+        ag_send(m, p, 2, 4 + 2 * l, own, toward(p, 2, 1))
+        ag_send(m, p, 2, 5 + 2 * l, own, toward(p, 2, 3))
 
     def ag_three_forward(m, p, l):
         second = turned(p, 1, l)
-        ag_wait(m, p, 7 + 4 * l, line(p, second, turned(p, 2, 3)), toward(p, 2, 3))
-        ag_send(m, p, 9 + 4 * l, line(p, second, turned(p, 2, 3), 0), toward(p, 2, 1))
-        ag_wait(m, p, 8 + 4 * l, line(p, second, turned(p, 2, 1)), toward(p, 2, 1))
-        ag_send(m, p, 10 + 4 * l, line(p, second, turned(p, 2, 1), 1), toward(p, 2, 3))
+        ag_wait(m, p, 4 + 2 * l, line(p, second, turned(p, 2, 3)))
+        ag_send(m, p, 2, 12, line(p, second, turned(p, 2, 3), 0), toward(p, 2, 1))
+        ag_wait(m, p, 5 + 2 * l, line(p, second, turned(p, 2, 1)))
+        ag_send(m, p, 2, 12, line(p, second, turned(p, 2, 1), 1), toward(p, 2, 3))
 
     def ag_three_last(m, p):
-        for l in range(4):
-            second = turned(p, 1, l)
-            ag_wait(m, p, 9 + 4 * l, line(p, second, turned(p, 2, 2), 0), toward(p, 2, 3))
-            ag_wait(m, p, 10 + 4 * l, line(p, second, turned(p, 2, 2), 1), toward(p, 2, 1))
-
-    def cols_of(p):
-        return pl.ds(OFFSETS[p], WIDTHS[p])
+        ag_wait(m, p, 12, place(p, FULL, FULL, turned(p, 2, 2)))
 
     def wide(v, w=HALF):
         return jnp.concatenate([v] * (w // 128), axis=1)
@@ -274,38 +267,43 @@
                 v[rows, cols] = st
             return st
 
-        ends[tm, :, cols] = lax.fori_loop(0, T // 4, body, jnp.zeros((PAIR, WIDTHS[p]), F32))
-
-    def ends_copy(n, ends, p, slot, d, dev):
+        last = lax.fori_loop(0, T // 4, body, jnp.zeros((PAIR, WIDTHS[p]), F32))
+        ends[tm, :, cols] = last.astype(BF16)
+
+    def ends_copy(n, ends, p, slots, dev):
         cols = pl.ds(0, HALF) if p is None else cols_of(p)
-        ref = ends.at[slot, :, cols]
-        return remote(ref, ref, pre_ss.at[n, d], pre_rs.at[n, slot], dev)
+        ref = ends.at[slots, :, cols]
+        return remote(ref, ref, pre_ss.at[n], pre_rs.at[n], dev)
 
     def prefix_send(n, ends, p, forward):
         for d in range(TM - 1, 0, -1):
             to = tm + d if forward else tm - d
 
             @pl.when(to < TM if forward else to >= 0)
-            def _(d=d, to=to):
-                ends_copy(n, ends, p, tm, d, {"tm": to, "batch": batch}).start()
+            def _(to=to):
+                ends_copy(n, ends, p, tm, {"tm": to, "batch": batch}).start()
+
+    def prefix_wait(n, ends, p, count, arrived):
+        for k in range(1, TM):
+
+            @pl.when(count == k)
+            def _(k=k):
+                copies = ends_copy(n, ends, p, pl.ds(0, k), partner)
+                copies.wait_recv() if arrived else copies.wait_send()
 
     def prefix_take(n, ends, p, forward):
-        cols = pl.ds(0, HALF) if p is None else cols_of(p)
-        carry[:, cols] = jnp.zeros_like(carry[:, cols])
-        for j in range(TM - 1) if forward else range(TM - 1, 0, -1):
-
-            @pl.when(j < tm if forward else j > tm)
-            def _(j=j):
-                ends_copy(n, ends, p, j, 0, {"tm": j, "batch": batch}).wait_recv()
-                carry[:, cols] = dall[j, :, cols] * carry[:, cols] + ends[j, :, cols]
+        cols, w = (pl.ds(0, HALF), HALF) if p is None else (cols_of(p), WIDTHS[p])
+        count = tm if forward else TM - 1 - tm
+        prefix_wait(n, ends, p, count, True)
+
+        def body(i, v):
+            j = i if forward else TM - 1 - i
+            return dall[j, :, cols] * v + ends[j, :, cols].astype(F32)
+
+        carry[:, cols] = lax.fori_loop(0, count, body, jnp.zeros((PAIR, w), F32))
 
     def prefix_drain(n, ends, p, forward):
-        for d in range(1, TM):
-            to = tm + d if forward else tm - d
-
-            @pl.when(to < TM if forward else to >= 0)
-            def _(d=d, to=to):
-                ends_copy(n, ends, p, tm, d, {"tm": to, "batch": batch}).wait_send()
+        prefix_wait(n, ends, p, TM - 1 - tm if forward else tm, False)
 
     def quality(v, heads, p, fresh, slope):
         cols, w = cols_of(p), WIDTHS[p]
@@ -349,26 +347,23 @@
         a0, a1 = lax.fori_loop(0, T // 8, body, (zero, zero))
         q_s[slot, 0] = a0
         q_s[slot, 1] = a1
-        send(q_s.at[slot], q_r.at[slot], d2d_ss.at[9 + slot], d2d_rs.at[9 + slot], partner)
+        send(q_s.at[slot], q_r.at[slot], d2d_ss.at[5 + slot], d2d_rs.at[5 + slot], partner)
 
     def quality_sum(slot):
         remote(
-            q_s.at[slot], q_r.at[slot], d2d_ss.at[9 + slot], d2d_rs.at[9 + slot], partner
+            q_s.at[slot], q_r.at[slot], d2d_ss.at[5 + slot], d2d_rs.at[5 + slot], partner
         ).wait_recv()
         return [(q_s[slot, k] + q_r[slot, k]) * (H ** (-0.5)) for k in range(2)]
 
     for m in range(2):
+        w_half_in(m)
         for p in range(3):
-            w_half_in(m, p)
             ag_one(m, p)
     for p in range(3):
         ag_one_in(0, p)
         ag_two(0, p)
         ag_three(0, p, 0)
-    for p in range(3):
-        ag_one_in(1, p)
-        ag_two(1, p)
-    remote(pk_m, pk_i, d2d_ss.at[6], d2d_rs.at[6], partner).wait_recv()
+    remote(pk_m, pk_i, d2d_ss.at[2], d2d_rs.at[2], partner).wait_recv()
     step8 = pk_m[0] + pk_i[0]
     rew8 = pk_m[1] + pk_i[1]
     logp8 = pk_m[2] + pk_i[2]
@@ -381,7 +376,7 @@
     sf[tm, 1] = jnp.broadcast_to(1.0 - jnp.max(rst8, axis=1, keepdims=True), (PAIR, 128))
     for d in range(1, TM):
         dev = {"tm": lax.rem(tm + d, TM), "batch": batch}
-        send(sf.at[tm], sf.at[tm], pre_ss.at[0, d], pre_rs.at[0, tm], dev)
+        remote(sf.at[tm], sf.at[tm], pre_ss.at[0], pre_rs.at[0], dev).start()
 
     spread_lanes(bc0, step8)
     spread_lanes(bc1, keep8)
@@ -402,48 +397,48 @@
         ag_three(0, p, 3)
         ag_three(0, p, 1)
     for p in range(3):
+        ag_one_in(1, p)
+        ag_two(1, p)
+    local[0].wait()
+    remote(nxt, xr_n.at[other_half, :], d2d_ss.at[3], d2d_rs.at[3], partner).wait_recv()
+    permute_next()
+    for p in range(3):
         ag_three_forward(0, p, 0)
-    local[0].wait()
-    remote(nxt, xr_n.at[other_half, :], d2d_ss.at[7], d2d_rs.at[7], partner).wait_recv()
-    permute_next()
+    for p in range(3):
+        ag_two_last(0, p)
+        ag_three(0, p, 2)
+    for l in (3, 1):
+        for p in range(3):
+            ag_three_forward(0, p, l)
     for p in range(3):
         ag_two_forward(1, p)
         ag_three(1, p, 0)
-    for p in range(3):
-        ag_two_last(0, p)
-        ag_three(0, p, 2)
     def tails(i, prod):
         t = T - 1 - i
         tp[at_t(t), :] = prod
         return prod * cc[at_t(t), :]
 
     lax.fori_loop(0, T, tails, jnp.ones((PAIR, HALF), F32))
-    local[1].wait()
-    remote(obs, xr_o.at[other_half, :], d2d_ss.at[8], d2d_rs.at[8], partner).wait_recv()
-    for l in (3, 1):
-        for p in range(3):
-            ag_three_forward(0, p, l)
-    for p in range(3):
+    for p in range(3):
+        ag_three_forward(0, p, 2)
         ag_three(1, p, 3)
         ag_three(1, p, 1)
+    local[1].wait()
+    remote(obs, xr_o.at[other_half, :], d2d_ss.at[4], d2d_rs.at[4], partner).wait_recv()
+    permute_obs(0, 4)
+    for p in range(3):
         ag_two_last(1, p)
-    permute_obs(0, 4)
-    for p in range(3):
-        ag_three_forward(0, p, 2)
         ag_three(1, p, 2)
-    permute_obs(4, 8)
-
-    for d in range(1, TM):
-        j = lax.rem(tm + d, TM)
-        dev = {"tm": j, "batch": batch}
-        remote(sf.at[j], sf.at[j], pre_ss.at[0, d], pre_rs.at[0, j], dev).wait_recv()
+    sums = remote(
+        sf.at[pl.ds(0, TM - 1)], sf.at[pl.ds(0, TM - 1)], pre_ss.at[0], pre_rs.at[0], partner
+    )
+    sums.wait_recv()
 
     def block_decay(j, _):
         dall[j] = jnp.exp(wide(sf[j, 0]) * ld8) * wide(sf[j, 1])
         return 0
 
     lax.fori_loop(0, TM, block_decay, 0)
-
     for p in range(3):
         ag_three_forward(1, p, 0)
     for p in PARTS[:2]:
@@ -457,23 +452,19 @@
         project(0, p, xp_n, vt)
         scan(vt, p, ends_t)
     prefix_send(1, ends_t, None, True)
-    for l in (1, 2):
-        for p in range(3):
-            ag_three_forward(1, p, l)
+    for p in range(3):
+        ag_three_forward(1, p, 1)
+    permute_obs(4, 8)
+    for p in range(3):
+        ag_three_forward(1, p, 2)
+    prefix_take(1, ends_t, None, True)
+    for p in PARTS:
+        quality(vt, tgh, p, p == PARTS[0], False)
+    quality_send(0)
     ag_three_last(1, PARTS[0])
     project(1, PARTS[0], xp_o, vo)
     scan(vo, PARTS[0], ends_o)
     prefix_send(2 + PARTS[0], ends_o, PARTS[0], True)
-    prefix_take(1, ends_t, None, True)
-    for p in PARTS:
-        quality(vt, tgh, p, p == PARTS[0], False)
-    quality_send(0)
-    for p in PARTS[1:]:
-        ag_three_last(1, p)
-    for p in PARTS[1:]:
-        project(1, p, xp_o, vo)
-        scan(vo, p, ends_o)
-        prefix_send(2 + p, ends_o, p, True)
     tq = quality_sum(0)
     value8 = jnp.minimum(tq[0], tq[1]) - ENTROPY_COEFF * logp8
     nb_s[0] = rew8
@@ -481,6 +472,14 @@
     nb_s[2] = keep8
     before = {"tm": lax.rem(tm + TM - 1, TM), "batch": batch}
     send(nb_s, nb_r, nb_sem.at[0], nb_sem.at[1], before)
+    ag_three_last(1, PARTS[1])
+    project(1, PARTS[1], xp_o, vo)
+    scan(vo, PARTS[1], ends_o)
+    prefix_send(2 + PARTS[1], ends_o, PARTS[1], True)
+    ag_three_last(1, PARTS[2])
+    project(1, PARTS[2], xp_o, vo)
+    scan(vo, PARTS[2], ends_o)
+    prefix_send(2 + PARTS[2], ends_o, PARTS[2], True)
     prefix_take(2 + PARTS[0], ends_o, PARTS[0], True)
     quality(vo, onh, PARTS[0], True, True)
 
@@ -530,7 +529,8 @@
                 adj = cc[rows, cols] * adj
             return adj
 
-        lv[tm, :, cols] = lax.fori_loop(0, T // 4, back, jnp.zeros((PAIR, w), F32))
+        leaving = lax.fori_loop(0, T // 4, back, jnp.zeros((PAIR, w), F32))
+        lv[tm, :, cols] = leaving.astype(BF16)
         prefix_send(5 + p, lv, p, False)
 
     def finish(p):
@@ -554,14 +554,20 @@
         v = jnp.dot(lhs, du[:, cols_of(p)], preferred_element_type=F32)
         gg[p][where] = v.reshape(4, 4, 32, WIDTHS[p])
 
-    def rs_copy(p, j, src, dst, dev):
-        n = p * RS_SEMS + j
-        return remote(src, dst, rs_ss.at[n], rs_rs.at[n], dev)
-
-    def rs_send(p, j, src, dst, dev):
-        copy = rs_copy(p, j, src, dst, dev)
-        copy.start()
-        pending.append(copy)
+    def rs_copy(p, k, j, src, dst, dev):
+        return remote(src, dst, rs_ss.at[p * 3 + k], rs_rs.at[p * RS_SEMS + j], dev)
+
+    def rs_half(p, s, h, dev):
+        return rs_copy(p, 0, 2 * s + h, snd_h[p].at[s, h], rcv_h[p].at[s, h], dev)
+
+    def rs_whole(p, s, h, dev):
+        return rs_copy(p, 1, 10 + s, snd_w[p].at[s, h], rcv_w[p].at[s, h], dev)
+
+    def rs_drain(p):
+        for k, (src, dst) in enumerate(
+            ((snd_h[p], rcv_h[p]), (snd_w[p], rcv_w[p]), (snd_b[p], rcv_b[p]))
+        ):
+            rs_copy(p, k, 0, src, dst, partner).wait_send()
 
     def rs_ref(p, s, d, h=None):
         if s < 4:
@@ -574,27 +580,18 @@
     def rs_opposite(p, s):
         for h, d in ((0, 3), (1, 1)):
             snd_h[p][s, h] = gg[p][rs_ref(p, s, 2, h)].astype(BF16)
-            rs_send(
-                p, 4 * s + h, snd_h[p].at[s, h], rcv_h[p].at[s, h], toward(p, rs_axis(s), d)
-            )
+            rs_half(p, s, h, toward(p, rs_axis(s), d)).start()
 
     def rs_neighbour(p, s, h):
         d = (3, 1)[h]
-        rs_copy(
-            p, 4 * s + h, snd_h[p].at[s, h], rcv_h[p].at[s, h], toward(p, rs_axis(s), 4 - d)
-        ).wait_recv()
+        rs_half(p, s, h, partner).wait_recv()
         with_recv = gg[p][rs_ref(p, s, d, h)] + rcv_h[p][s, h].astype(F32)
         snd_w[p][s, h, pl.ds(2 * h, 2)] = with_recv.astype(BF16)
         snd_w[p][s, h, pl.ds(2 - 2 * h, 2)] = gg[p][rs_ref(p, s, d, 1 - h)].astype(BF16)
-        rs_send(
-            p, 4 * s + 2 + h, snd_w[p].at[s, h], rcv_w[p].at[s, h], toward(p, rs_axis(s), d)
-        )
+        rs_whole(p, s, h, toward(p, rs_axis(s), d)).start()
 
     def rs_sum(p, s):
-        for h, d in ((0, 1), (1, 3)):
-            rs_copy(
-                p, 4 * s + 2 + h, snd_w[p].at[s, h], rcv_w[p].at[s, h], toward(p, rs_axis(s), d)
-            ).wait_recv()
+        rs_copy(p, 1, 10 + s, snd_w[p].at[s], rcv_w[p].at[s], partner).wait_recv()
         own = rs_ref(p, s, 0)
         both = rcv_w[p][s, 0].astype(F32) + rcv_w[p][s, 1].astype(F32)
         gg[p][own] = gg[p][own] + both
@@ -603,16 +600,14 @@
         for d in (2, 1, 3):
             block = gg[p][place(p, turned(p, 0, d), turned(p, 1, 0), turned(p, 2, 0))]
             snd_b[p][d - 1] = block.astype(BF16)
-            rs_send(p, 19 + d, snd_b[p].at[d - 1], rcv_b[p].at[d - 1], toward(p, 0, d))
+            rs_copy(p, 2, 15, snd_b[p].at[d - 1], rcv_b[p].at[d - 1], toward(p, 0, d)).start()
 
     def rs_one_sum(p):
+        rs_copy(p, 2, 15, snd_b[p], rcv_b[p], partner).wait_recv()
         v = gg[p][y, x, z]
-        for d in (1, 3, 2):
-            rs_copy(
-                p, 19 + d, snd_b[p].at[d - 1], rcv_b[p].at[d - 1], toward(p, 0, 4 - d)
-            ).wait_recv()
-            v = v + rcv_b[p][d - 1].astype(F32)
-        gg[p][y, x, z] = v * SCALE
+        for d in range(3):
+            v = v + rcv_b[p][d].astype(F32)
+        gg[p][y, x, z] = v
 
     for p in PARTS:
         finish(p)
@@ -647,17 +642,23 @@
 
     for p in range(3):
         gx_s[:, cols_of(p)] = gg[p][y, x, z, other_rows, :]
-    send(gx_s, gx_r, d2d_ss.at[11], d2d_rs.at[11], partner)
+    send(gx_s, gx_r, d2d_ss.at[7], d2d_rs.at[7], partner)
     for p in range(3):
         cols = pl.ds(pl.multiple_of(c * HALF + OFFSETS[p], 128), WIDTHS[p])
         gw[:, cols] = gg[p][y, x, z, own_rows, :]
-    remote(gx_s, gx_r, d2d_ss.at[11], d2d_rs.at[11], partner).wait_recv()
+    remote(gx_s, gx_r, d2d_ss.at[7], d2d_rs.at[7], partner).wait_recv()
     gw[:, theirs] = gx_r[...]
 
     prefix_drain(1, ends_t, None, True)
     for p in range(3):
         prefix_drain(2 + p, ends_o, p, True)
         prefix_drain(5 + p, lv, p, False)
+    for p in range(3):
+        ag_drain(0, p)
+        ag_drain(1, p)
+        rs_drain(p)
+    remote(wst, wst, d2d_ss.at[0], d2d_rs.at[0], partner).wait_send()
+    sums.wait_send()
     for copy in pending:
         copy.wait_send()
 
@@ -676,7 +677,7 @@
         *[pltpu.VMEM((3, 32, w), BF16) for w in WIDTHS],
     ]
     big = pltpu.VMEM((ROWS, HALF), F32)
-    ends = pltpu.VMEM((TM, PAIR, HALF), F32)
+    ends = pltpu.VMEM((TM, PAIR, HALF), BF16)
     narrow = pltpu.VMEM((ROWS, 128), F32)
     scratch = [
         pltpu.VMEM((ROWS, D), BF16), pltpu.VMEM((ROWS, D), BF16),
@@ -686,7 +687,7 @@
         pltpu.VMEM((6, PAIR, 128), F32), pltpu.VMEM((6, PAIR, 128), F32),
         narrow, narrow, narrow, narrow,
         big, big, big, big, big, big,
-        pltpu.VMEM((TM, 2, PAIR, 128), F32), ends, ends, ends, ends,
+        pltpu.VMEM((TM, 2, PAIR, 128), F32), pltpu.VMEM((TM, PAIR, HALF), F32), ends, ends, ends,
         pltpu.VMEM((PAIR, HALF), F32),
         pltpu.VMEM((2, 2, PAIR, 128), F32), pltpu.VMEM((2, 2, PAIR, 128), F32),
         pltpu.VMEM((3, PAIR, 128), F32), pltpu.VMEM((3, PAIR, 128), F32),
@@ -694,15 +695,15 @@
         *[pltpu.VMEM((4, 4, 4, 32, w), F32) for w in WIDTHS],
         *staged, *staged,
         pltpu.VMEM((16, HALF), F32), pltpu.VMEM((16, HALF), F32),
-        pltpu.SemaphoreType.DMA((6 * AG_SEMS,)), pltpu.SemaphoreType.DMA((6 * AG_SEMS,)),
-        pltpu.SemaphoreType.DMA((3 * RS_SEMS,)), pltpu.SemaphoreType.DMA((3 * RS_SEMS,)),
-        pltpu.SemaphoreType.DMA((8, TM)), pltpu.SemaphoreType.DMA((8, TM)),
+        pltpu.SemaphoreType.DMA((18,)), pltpu.SemaphoreType.DMA((6 * AG_SEMS,)),
+        pltpu.SemaphoreType.DMA((9,)), pltpu.SemaphoreType.DMA((3 * RS_SEMS,)),
+        pltpu.SemaphoreType.DMA((8,)), pltpu.SemaphoreType.DMA((8,)),
         pltpu.SemaphoreType.DMA((2,)),
-        pltpu.SemaphoreType.DMA((12,)), pltpu.SemaphoreType.DMA((12,)),
+        pltpu.SemaphoreType.DMA((8,)), pltpu.SemaphoreType.DMA((8,)),
         pltpu.SemaphoreType.DMA((2,)),
     ]
     rows_b, span, width = obs_feats.shape
-    grad_w, returns = pl.pallas_call(
+    grad, returns = pl.pallas_call(
         kernel,
         name="critic_step",
         out_shape=(
@@ -720,6 +721,7 @@
         online_w, target_w, log_decay[None], step_scale, online_heads, target_heads,
         reward, next_action_log_prob, resets, horizon, burn_in,
     )
+    grad_w = grad * SCALE
     new_target = (1.0 - POLYAK_RATE) * target_w + POLYAK_RATE * (online_w - STEP_SIZE * grad_w)
     return grad_w, new_target, returns
 

time: 117 us -> 106 us (0.906)
  Pallas kernels: 113 us -> 103 us
    pallas_call x1, Pallas kernels: 113 us -> 103 us  [shards(): pl.pallas_call(kernel, name='critic_step', out_shape=(jax.ShapeDtypeStruc...]
where the time goes in v2:
time: 106 us
  Pallas kernels  103 us (97%)
  other arithmetic  1.64 us (2%)
  local copies, waits for them, and re-layouts  1.24 us (1%)
    pallas_call x1, Pallas kernels, shards(): pl.pallas_call(kernel, name='critic_step', out_shape=(jax.ShapeDtypeStruc...  103 us

profile of v2, /device:TPU:1, one launch (start us, length us, event | category | flops | bytes accessed | tf_op | source)
XLA Modules:
  0.0 106.3 jit_solution(4162965729843067731)
XLA Ops:
  0.6 0.0 copy-start
  0.6 0.0 copy-start.1
  0.7 102.7 %critic_step.1 = (f32[16,2048]{1,0:T(8,128)}, f32[4,64]{1,0:T(4,128)}) custom-call(bf16[256,2048]{1,0:T(8,128)(2,1)} %bitcast.3, bf16[256,2048]{1,0:T(8,128)(2,1)} %bitcast.4, f32[16,2048]{1,0:T(8,128)} %onw.1, f32[16,2048]{1,0:T(8,128)} %tgw.1, f32[1,2048]{1,0:T(1,128)} %bitcast.5, f32[4,64]{1,0:T(4,128)} %step.1, f32[2,2048]{1,0:T(2,128)} %onh.1, ...), custom_call_target="tpu_custom_call" | custom-call | tf_op jit(solution)/shard_map/critic_step/pallas_call | solution.py:706
  103.4 0.0 copy-done
  103.4 0.0 copy-done.1
  103.4 1.6 %multiply_add_fusion = (f32[16,2048]{1,0:T(8,128)}, f32[16,2048]{1,0:T(8,128)}) fusion(f32[16,2048]{1,0:T(8,128)S(1)} %copy-done, f32[16,2048]{1,0:T(8,128)} %get-tuple-element.5, f32[16,2048]{1,0:T(8,128)S(1)} %copy-done.1), kind=kLoop, calls=%fused_computation | loop fusion | flops 196608 | bytes 655360 | tf_op jit(solution)/shard_map/add | solution.py:725
  105.0 0.0 copy-start.2
  105.0 0.7 copy-done.2
  105.7 0.6 copy.17
Async XLA Ops:
  0.6 102.7 %copy-start = (f32[16,2048]{1,0:T(8,128)S(1)}, f32[16,2048]{1,0:T(8,128)}, u32[]{:S(2)}) copy-start(f32[16,2048]{1,0:T(8,128)} %onw.1) | copy-start | bytes 393220
  0.6 102.7 %copy-start.1 = (f32[16,2048]{1,0:T(8,128)S(1)}, f32[16,2048]{1,0:T(8,128)}, u32[]{:S(2)}) copy-start(f32[16,2048]{1,0:T(8,128)} %tgw.1) | copy-start | bytes 393220
  105.0 0.7 copy-start.2

commit v3 on v2

--- a/solution.py
+++ b/solution.py
@@ -22,30 +22,34 @@
 PAIR = 8
 ROWS = T * PAIR
 TM = 16
+VMEM_LIMIT = 56
 SCALE = D ** (-0.5)
 
-WIDTHS = (384, 384, 256)
-OFFSETS = (0, 384, 768)
+WIDTHS_T = (384, 256, 384)
+OFFSETS_T = (0, 384, 640)
+WIDTHS = (256, 384, 384)
+OFFSETS = (0, 256, 640)
 ORDERS = (("z", "x", "y"), ("y", "z", "x"), ("x", "y", "z"))
-PARTS = (2, 0, 1)
+PARTS = (0, 2, 1)
 AG_SEMS = 13
 RS_SEMS = 16
 LINES = (2, 3, 1, 0)
 
 
 def kernel(
-    obs, nxt, onw, tgw, ld, step, onh, tgh, rew, logp, rst, hor, burn,
+    obs, nxt, onw_in, tgw_in, ld_in, step_in, onh_in, tgh_in, rew_in, logp_in, rst_in, hor, burn,
     gw, ret,
+    onw, tgw, ld, step, onh, tgh, rew, logp, rst,
     xr_o, xr_n, xp_o, xp_n, xt, wst,
     wt0, wt1, wt2, wo0, wo1, wo2,
     pk_m, pk_i, bc0, bc1, qa0, qa1, cc, ss, pf, tp, vt, vo,
-    sf, dall, ends_t, ends_o, lv, carry,
+    sf, dfor, dback, ends_t, ends_o, lv, carry,
     q_s, q_r, nb_s, nb_r, du,
     g0, g1, g2,
     sh0, sh1, sh2, sw0, sw1, sw2, sb0, sb1, sb2,
     rh0, rh1, rh2, rw0, rw1, rw2, rb0, rb1, rb2,
     gx_s, gx_r,
-    ag_ss, ag_rs, rs_ss, rs_rs, pre_ss, pre_rs, loc_sem, d2d_ss, d2d_rs, nb_sem,
+    ag_ss, ag_rs, rs_ss, rs_rs, pre_ss, pre_rs, loc_sem, in_sem, d2d_ss, d2d_rs, nb_sem,
 ):
     tm = lax.axis_index("tm")
     batch = lax.axis_index("batch")
@@ -76,6 +80,30 @@
         copy.start()
         pending.append(copy)
 
+    barrier = pltpu.get_barrier_semaphore()
+    peers = [partner] + [device(z=lax.rem(z + d, 4)) for d in range(1, 4)]
+    peers += [{"tm": lax.rem(tm + d, TM), "batch": batch} for d in range(1, TM)]
+    for dev in peers:
+        pl.semaphore_signal(barrier, inc=1, device_id=dev, device_id_type=MESH)
+
+    own_half = pl.ds(pl.multiple_of(c * 256, 256), 256)
+    other_half = pl.ds(pl.multiple_of(other * 256, 256), 256)
+    loads = [
+        pltpu.make_async_copy(src, dst, in_sem.at[i])
+        for i, (src, dst) in enumerate((
+            (tgw_in, tgw), (onw_in, onw), (step_in, step), (rew_in, rew), (logp_in, logp),
+            (rst_in, rst), (ld_in, ld), (onh_in, onh), (tgh_in, tgh),
+        ))
+    ]
+    local = [
+        pltpu.make_async_copy(nxt, xr_n.at[own_half, :], loc_sem.at[0]),
+        pltpu.make_async_copy(obs, xr_o.at[own_half, :], loc_sem.at[1]),
+    ]
+    for copy in loads + local:
+        copy.start()
+    for copy in loads:
+        copy.wait()
+
     mine = pl.ds(pl.multiple_of(c * HALF, HALF), HALF)
     theirs = pl.ds(pl.multiple_of(other * HALF, HALF), HALF)
     own_rows = pl.ds(pl.multiple_of(c * 16, 16), 16)
@@ -83,7 +111,8 @@
     for m, w in enumerate((tgw, onw)):
         wst[m] = w[:, theirs].astype(BF16)
         for p in range(3):
-            cols = pl.ds(pl.multiple_of(c * HALF + OFFSETS[p], 128), WIDTHS[p])
+            off = (OFFSETS_T, OFFSETS)[m][p]
+            cols = pl.ds(pl.multiple_of(c * HALF + off, 128), (WIDTHS_T, WIDTHS)[m][p])
             wb[m][p][y, x, z, own_rows, :] = w[:, cols].astype(BF16)
 
     row8 = lax.broadcasted_iota(jnp.int32, (PAIR, 128), 0)
@@ -106,31 +135,20 @@
     pk_m[4] = hz
     pk_m[5] = bz
 
-    own_half = pl.ds(pl.multiple_of(c * 256, 256), 256)
-    other_half = pl.ds(pl.multiple_of(other * 256, 256), 256)
-    local = [
-        pltpu.make_async_copy(nxt, xr_n.at[own_half, :], loc_sem.at[0]),
-        pltpu.make_async_copy(obs, xr_o.at[own_half, :], loc_sem.at[1]),
-    ]
-    for copy in local:
-        copy.start()
-
-    barrier = pltpu.get_barrier_semaphore()
-    peers = [partner] + [device(z=lax.rem(z + d, 4)) for d in range(1, 4)]
-    peers += [{"tm": lax.rem(tm + d, TM), "batch": batch} for d in range(1, TM)]
-    for dev in peers:
-        pl.semaphore_signal(barrier, inc=1, device_id=dev, device_id_type=MESH)
     pl.semaphore_wait(barrier, len(peers))
 
     def w_half(m, p):
-        src, dst = wst.at[m, :, cols_of(p)], wb[m][p].at[y, x, z, own_rows, :]
+        src, dst = wst.at[m, :, cols_of(p, m)], wb[m][p].at[y, x, z, own_rows, :]
         return remote(src, dst, d2d_ss.at[0], d2d_rs.at[m], partner)
 
     def w_half_in(m):
         remote(wst.at[m], wst.at[m], d2d_ss.at[0], d2d_rs.at[m], partner).wait_recv()
 
-    def cols_of(p):
-        return pl.ds(OFFSETS[p], WIDTHS[p])
+    def width(m, p):
+        return (WIDTHS_T, WIDTHS)[m][p]
+
+    def cols_of(p, m=1):
+        return pl.ds((OFFSETS_T, OFFSETS)[m][p], width(m, p))
 
     for m in range(2):
         for p in range(3):
@@ -159,6 +177,9 @@
         n = m * 3 + p
         return remote(ref, ref, ag_ss.at[n * 3 + k], ag_rs.at[n * AG_SEMS + j], dev)
 
+    def ag_end(m, p, l):
+        return 12 + l if (m, p) == (1, 2) else 12
+
     def ag_send(m, p, k, j, where, dev):
         ag_copy(m, p, k, j, where, dev).start()
 
@@ -180,9 +201,21 @@
         ag_wait(m, p, 0, (0, 0, pl.ds(0, 3)))
 
     def ag_two(m, p):
-        own = line(p, turned(p, 1, 0), turned(p, 2, 0))
-        ag_send(m, p, 1, 1, own, toward(p, 1, 1))
-        ag_send(m, p, 1, 2, own, toward(p, 1, 3))
+        for d in (1, 3, 2):
+            where = place(p, turned(p, 0, d), turned(p, 1, 0), turned(p, 2, 0))
+            ag_send(m, p, 1, 1, where, toward(p, 1, 1))
+            ag_send(m, p, 1, 2, where, toward(p, 1, 3))
+
+    def ag_three_own(m, p):
+        for d in (1, 3, 2):
+            where = place(p, turned(p, 0, d), turned(p, 1, 0), turned(p, 2, 0))
+            ag_send(m, p, 2, 4, where, toward(p, 2, 1))
+            ag_send(m, p, 2, 5, where, toward(p, 2, 3))
+
+    def ag_early(m, p):
+        for k in (1, 2):
+            ag_send(m, p, k, 3 * k - 2, (y, x, z), toward(p, k, 1))
+            ag_send(m, p, k, 3 * k - 1, (y, x, z), toward(p, k, 3))
 
     def ag_two_forward(m, p):
         q3 = turned(p, 2, 0)
@@ -202,12 +235,15 @@
     def ag_three_forward(m, p, l):
         second = turned(p, 1, l)
         ag_wait(m, p, 4 + 2 * l, line(p, second, turned(p, 2, 3)))
-        ag_send(m, p, 2, 12, line(p, second, turned(p, 2, 3), 0), toward(p, 2, 1))
+        ag_send(m, p, 2, ag_end(m, p, l), line(p, second, turned(p, 2, 3), 0), toward(p, 2, 1))
         ag_wait(m, p, 5 + 2 * l, line(p, second, turned(p, 2, 1)))
-        ag_send(m, p, 2, 12, line(p, second, turned(p, 2, 1), 1), toward(p, 2, 3))
+        ag_send(m, p, 2, ag_end(m, p, l), line(p, second, turned(p, 2, 1), 1), toward(p, 2, 3))
 
     def ag_three_last(m, p):
         ag_wait(m, p, 12, place(p, FULL, FULL, turned(p, 2, 2)))
+
+    def ag_line_last(l):
+        ag_wait(1, 2, 12 + l, line(2, turned(2, 1, l), turned(2, 2, 2)))
 
     def wide(v, w=HALF):
         return jnp.concatenate([v] * (w // 128), axis=1)
@@ -250,15 +286,37 @@
     def project(m, p, xp, v):
         def tile(i, _):
             rows = pl.ds(pl.multiple_of(i * 256, 256), 256)
-            w = wb[m][p][...].reshape(D, WIDTHS[p])
+            w = wb[m][p][...].reshape(D, width(m, p))
             acc = jnp.dot(xp[rows, :], w, preferred_element_type=F32)
-            v[rows, cols_of(p)] = acc * SCALE
+            v[rows, cols_of(p, m)] = acc * SCALE
             return 0
 
         lax.fori_loop(0, ROWS // 256, tile, 0)
 
-    def scan(v, p, ends):
-        cols = cols_of(p)
+    def project_planes(p, planes, fresh):
+        axis = 1 if p == 2 else 2
+        qs = [turned(p, axis, d) for d in planes]
+
+        def tile(i, _):
+            rows = pl.ds(pl.multiple_of(i * 256, 256), 256)
+            acc = None if fresh else vo[rows, cols_of(p)]
+            for q in qs:
+                where = place(p, FULL, q, FULL) if p == 2 else place(p, FULL, FULL, q)
+                w = wb[1][p][where].reshape(512, WIDTHS[p])
+                if p == 1:
+                    starts = [pl.multiple_of((k * 4 + q) * 128, 128) for k in range(4)]
+                    lhs = jnp.concatenate([xp_o[rows, pl.ds(k, 128)] for k in starts], axis=1)
+                else:
+                    lhs = xp_o[rows, pl.ds(pl.multiple_of(q * 512, 512), 512)]
+                v = jnp.dot(lhs, w, preferred_element_type=F32) * SCALE
+                acc = v if acc is None else acc + v
+            vo[rows, cols_of(p)] = acc
+            return 0
+
+        lax.fori_loop(0, ROWS // 256, tile, 0)
+
+    def scan(m, v, p, ends):
+        cols = cols_of(p, m)
 
         def body(i, st):
             for k in range(4):
@@ -267,8 +325,8 @@
                 v[rows, cols] = st
             return st
 
-        last = lax.fori_loop(0, T // 4, body, jnp.zeros((PAIR, WIDTHS[p]), F32))
-        ends[tm, :, cols] = last.astype(BF16)
+        last = lax.fori_loop(0, T // 4, body, jnp.zeros((PAIR, width(m, p)), F32))
+        ends[tm, :, cols] = last
 
     def ends_copy(n, ends, p, slots, dev):
         cols = pl.ds(0, HALF) if p is None else cols_of(p)
@@ -293,21 +351,20 @@
 
     def prefix_take(n, ends, p, forward):
         cols, w = (pl.ds(0, HALF), HALF) if p is None else (cols_of(p), WIDTHS[p])
-        count = tm if forward else TM - 1 - tm
-        prefix_wait(n, ends, p, count, True)
-
-        def body(i, v):
-            j = i if forward else TM - 1 - i
-            return dall[j, :, cols] * v + ends[j, :, cols].astype(F32)
-
-        carry[:, cols] = lax.fori_loop(0, count, body, jnp.zeros((PAIR, w), F32))
+        prefix_wait(n, ends, p, tm if forward else TM - 1 - tm, True)
+        decay = dfor if forward else dback
+        v = jnp.zeros((PAIR, w), F32)
+        for j in range(TM - 1) if forward else range(TM - 1, 0, -1):
+            counted = jnp.where(j < tm if forward else j > tm, 1.0, 0.0)
+            v = decay[j, :, cols] * v + counted * ends[j, :, cols].astype(F32)
+        carry[:, cols] = v
 
     def prefix_drain(n, ends, p, forward):
         prefix_wait(n, ends, p, TM - 1 - tm if forward else tm, False)
 
-    def quality(v, heads, p, fresh, slope):
-        cols, w = cols_of(p), WIDTHS[p]
-        hcols = pl.ds(pl.multiple_of(c * HALF + OFFSETS[p], 128), w)
+    def quality(m, v, heads, p, fresh, slope):
+        cols, w = cols_of(p, m), width(m, p)
+        hcols = pl.ds(pl.multiple_of(c * HALF + (OFFSETS_T, OFFSETS)[m][p], 128), w)
         h0 = jnp.broadcast_to(heads[0:1, hcols], (PAIR, w))
         h1 = jnp.broadcast_to(heads[1:2, hcols], (PAIR, w))
         start = carry[:, cols]
@@ -319,32 +376,32 @@
             return out
 
         def body(i, _):
-            for k in range(4):
-                rows = at_t(i * 4 + k)
+            for k in range(8):
+                rows = at_t(i * 8 + k)
                 st = v[rows, cols] + pf[rows, cols] * start
                 sig = 1.0 / (1.0 + jnp.exp(-st))
                 act = st * sig
                 if slope:
-                    v[rows, cols] = (sig + act * (1.0 - sig)) * (H ** (-0.5))
+                    v[rows, cols] = sig + act * (1.0 - sig)
                 f0, f1 = fold(act * h0), fold(act * h1)
                 qa0[rows, :] = f0 if fresh else qa0[rows, :] + f0
                 qa1[rows, :] = f1 if fresh else qa1[rows, :] + f1
             return 0
 
-        lax.fori_loop(0, T // 4, body, 0)
+        lax.fori_loop(0, T // 8, body, 0)
 
     def quality_send(slot):
         def body(i, acc):
             a0, a1 = acc
-            for k in range(8):
-                rows = at_t(i * 8 + k)
-                here = lane8 == i * 8 + k
+            for k in range(16):
+                rows = at_t(i * 16 + k)
+                here = lane8 == i * 16 + k
                 a0 = jnp.where(here, jnp.sum(qa0[rows, :], axis=1, keepdims=True), a0)
                 a1 = jnp.where(here, jnp.sum(qa1[rows, :], axis=1, keepdims=True), a1)
             return a0, a1
 
         zero = jnp.zeros((PAIR, 128), F32)
-        a0, a1 = lax.fori_loop(0, T // 8, body, (zero, zero))
+        a0, a1 = lax.fori_loop(0, T // 16, body, (zero, zero))
         q_s[slot, 0] = a0
         q_s[slot, 1] = a1
         send(q_s.at[slot], q_r.at[slot], d2d_ss.at[5 + slot], d2d_rs.at[5 + slot], partner)
@@ -359,10 +416,26 @@
         w_half_in(m)
         for p in range(3):
             ag_one(m, p)
+        for p in range(3):
+            ag_early(m, p)
     for p in range(3):
         ag_one_in(0, p)
         ag_two(0, p)
-        ag_three(0, p, 0)
+    for p in range(3):
+        ag_three_own(0, p)
+    def clear(j, _):
+        @pl.when(j > tm)
+        def _():
+            ends_t[j] = jnp.zeros((PAIR, HALF), F32)
+            ends_o[j] = jnp.zeros((PAIR, HALF), F32)
+
+        @pl.when(j < tm)
+        def _():
+            lv[j] = jnp.zeros((PAIR, HALF), BF16)
+
+        return 0
+
+    lax.fori_loop(0, TM, clear, 0)
     remote(pk_m, pk_i, d2d_ss.at[2], d2d_rs.at[2], partner).wait_recv()
     step8 = pk_m[0] + pk_i[0]
     rew8 = pk_m[1] + pk_i[1]
@@ -393,17 +466,20 @@
 
     lax.fori_loop(0, T, factors, jnp.ones((PAIR, HALF), F32))
     for p in range(3):
+        ag_one_in(1, p)
+        ag_two(1, p)
+    for p in range(3):
         ag_two_forward(0, p)
         ag_three(0, p, 3)
         ag_three(0, p, 1)
-    for p in range(3):
-        ag_one_in(1, p)
-        ag_two(1, p)
     local[0].wait()
     remote(nxt, xr_n.at[other_half, :], d2d_ss.at[3], d2d_rs.at[3], partner).wait_recv()
     permute_next()
     for p in range(3):
         ag_three_forward(0, p, 0)
+    local[1].wait()
+    remote(obs, xr_o.at[other_half, :], d2d_ss.at[4], d2d_rs.at[4], partner).wait_recv()
+    permute_obs(0, 8)
     for p in range(3):
         ag_two_last(0, p)
         ag_three(0, p, 2)
@@ -412,7 +488,7 @@
             ag_three_forward(0, p, l)
     for p in range(3):
         ag_two_forward(1, p)
-        ag_three(1, p, 0)
+        ag_three_own(1, p)
     def tails(i, prod):
         t = T - 1 - i
         tp[at_t(t), :] = prod
@@ -423,9 +499,6 @@
         ag_three_forward(0, p, 2)
         ag_three(1, p, 3)
         ag_three(1, p, 1)
-    local[1].wait()
-    remote(obs, xr_o.at[other_half, :], d2d_ss.at[4], d2d_rs.at[4], partner).wait_recv()
-    permute_obs(0, 4)
     for p in range(3):
         ag_two_last(1, p)
         ag_three(1, p, 2)
@@ -435,7 +508,9 @@
     sums.wait_recv()
 
     def block_decay(j, _):
-        dall[j] = jnp.exp(wide(sf[j, 0]) * ld8) * wide(sf[j, 1])
+        v = jnp.exp(wide(sf[j, 0]) * ld8) * wide(sf[j, 1])
+        dfor[j] = jnp.where(j < tm, v, 1.0)
+        dback[j] = jnp.where(j > tm, v, 1.0)
         return 0
 
     lax.fori_loop(0, TM, block_decay, 0)
@@ -444,27 +519,42 @@
     for p in PARTS[:2]:
         ag_three_last(0, p)
         project(0, p, xp_n, vt)
-        scan(vt, p, ends_t)
+        scan(0, vt, p, ends_t)
     for p in range(3):
         ag_three_forward(1, p, 3)
     for p in PARTS[2:]:
         ag_three_last(0, p)
         project(0, p, xp_n, vt)
-        scan(vt, p, ends_t)
+        scan(0, vt, p, ends_t)
     prefix_send(1, ends_t, None, True)
     for p in range(3):
         ag_three_forward(1, p, 1)
-    permute_obs(4, 8)
     for p in range(3):
         ag_three_forward(1, p, 2)
+    for p in (0, 1):
+        project_planes(p, (0, 1, 3), True)
+    for l in (0, 3, 1):
+        ag_line_last(l)
+    project_planes(2, (0, 1, 3), True)
+    ag_three_last(1, 0)
+    project_planes(0, (2,), False)
+    scan(1, vo, PARTS[0], ends_o)
+    prefix_send(2 + PARTS[0], ends_o, PARTS[0], True)
+    ag_line_last(2)
+    project_planes(2, (2,), False)
+    scan(1, vo, PARTS[1], ends_o)
+    prefix_send(2 + PARTS[1], ends_o, PARTS[1], True)
+    ag_three_last(1, 1)
+    project_planes(1, (2,), False)
+    scan(1, vo, PARTS[2], ends_o)
+    prefix_send(2 + PARTS[2], ends_o, PARTS[2], True)
     prefix_take(1, ends_t, None, True)
     for p in PARTS:
-        quality(vt, tgh, p, p == PARTS[0], False)
+        quality(0, vt, tgh, p, p == PARTS[0], False)
     quality_send(0)
-    ag_three_last(1, PARTS[0])
-    project(1, PARTS[0], xp_o, vo)
-    scan(vo, PARTS[0], ends_o)
-    prefix_send(2 + PARTS[0], ends_o, PARTS[0], True)
+    prefix_take(2 + PARTS[0], ends_o, PARTS[0], True)
+    quality(1, vo, onh, PARTS[0], True, True)
+
     tq = quality_sum(0)
     value8 = jnp.minimum(tq[0], tq[1]) - ENTROPY_COEFF * logp8
     nb_s[0] = rew8
@@ -472,17 +562,10 @@
     nb_s[2] = keep8
     before = {"tm": lax.rem(tm + TM - 1, TM), "batch": batch}
     send(nb_s, nb_r, nb_sem.at[0], nb_sem.at[1], before)
-    ag_three_last(1, PARTS[1])
-    project(1, PARTS[1], xp_o, vo)
-    scan(vo, PARTS[1], ends_o)
-    prefix_send(2 + PARTS[1], ends_o, PARTS[1], True)
-    ag_three_last(1, PARTS[2])
-    project(1, PARTS[2], xp_o, vo)
-    scan(vo, PARTS[2], ends_o)
-    prefix_send(2 + PARTS[2], ends_o, PARTS[2], True)
-    prefix_take(2 + PARTS[0], ends_o, PARTS[0], True)
-    quality(vo, onh, PARTS[0], True, True)
-
+    for p in PARTS[1:]:
+        prefix_take(2 + p, ends_o, p, True)
+        quality(1, vo, onh, p, False, True)
+    quality_send(1)
     remote(nb_s, nb_r, nb_sem.at[0], nb_sem.at[1], before).wait_recv()
     inside = (lane8 >= T) & (lane8 < T + NMAX) & (tm < TM - 1)
 
@@ -506,13 +589,9 @@
     ret[...] = jnp.where(c == 0, total[:4, :T], total[4:, :T])
     weight = jnp.where((lane8 + tm * T).astype(F32) >= burn8, 1.0, 0.0)
 
-    for p in PARTS[1:]:
-        prefix_take(2 + p, ends_o, p, True)
-        quality(vo, onh, p, False, True)
-    quality_send(1)
     oq = quality_sum(1)
-    spread_lanes(bc0, weight * (oq[0] - total))
-    spread_lanes(bc1, weight * (oq[1] - total))
+    spread_lanes(bc0, weight * (oq[0] - total) * (H ** (-0.5)))
+    spread_lanes(bc1, weight * (oq[1] - total) * (H ** (-0.5)))
 
     for p in PARTS:
         cols, w = cols_of(p), WIDTHS[p]
@@ -616,20 +695,29 @@
     for p in PARTS:
         gradient(p, LINES[1])
         rs_opposite(p, LINES[1])
-    for i in range(4):
-        if i < 2:
-            for p in PARTS:
-                gradient(p, LINES[i + 2])
-                rs_opposite(p, LINES[i + 2])
-        for p in PARTS:
-            rs_neighbour(p, LINES[i], 0)
-            rs_neighbour(p, LINES[i], 1)
+    for p in PARTS:
+        rs_neighbour(p, LINES[0], 0)
+        rs_neighbour(p, LINES[0], 1)
+        gradient(p, LINES[2])
+        rs_opposite(p, LINES[2])
+    for p in PARTS:
+        rs_neighbour(p, LINES[1], 0)
+        rs_neighbour(p, LINES[1], 1)
+        gradient(p, LINES[3])
+        rs_opposite(p, LINES[3])
     for p in PARTS:
         rs_sum(p, LINES[0])
         rs_opposite(p, 4)
     for p in PARTS:
+        rs_neighbour(p, LINES[2], 0)
+        rs_neighbour(p, LINES[2], 1)
+    for p in PARTS:
         rs_sum(p, LINES[1])
         rs_neighbour(p, 4, 0)
+    for p in PARTS:
+        rs_neighbour(p, LINES[3], 0)
+        rs_neighbour(p, LINES[3], 1)
+    for p in PARTS:
         rs_sum(p, LINES[2])
         rs_neighbour(p, 4, 1)
     for p in PARTS:
@@ -663,31 +751,43 @@
         copy.wait_send()
 
 
+def update(grad, returns, onw, tgw, grad_w, new_target, returns_out):
+    g = grad[...] * SCALE
+    grad_w[...] = g
+    new_target[...] = (1.0 - POLYAK_RATE) * tgw[...] + POLYAK_RATE * (onw[...] - STEP_SIZE * g)
+    returns_out[...] = returns[...]
+
+
 def shards(
     obs_feats, next_feats, online_w, target_w, log_decay, step_scale, online_heads, target_heads,
     reward, next_action_log_prob, resets, horizon, burn_in,
 ):
     vmem = pl.BlockSpec(memory_space=pltpu.VMEM)
     smem = pl.BlockSpec(memory_space=pltpu.SMEM)
-    hbm = pl.BlockSpec(memory_space=pl.ANY)
-    weights = [pltpu.VMEM((4, 4, 4, 32, w), BF16) for w in WIDTHS]
+    hbm = pl.BlockSpec(memory_space=pltpu.HBM)
+    small = (
+        online_w, target_w, log_decay[None], step_scale, online_heads, target_heads,
+        reward, next_action_log_prob, resets,
+    )
+    weights = [pltpu.VMEM((4, 4, 4, 32, w), BF16) for w in WIDTHS_T + WIDTHS]
     staged = [
         *[pltpu.VMEM((5, 2, 2, 32, w), BF16) for w in WIDTHS],
         *[pltpu.VMEM((5, 2, 4, 32, w), BF16) for w in WIDTHS],
         *[pltpu.VMEM((3, 32, w), BF16) for w in WIDTHS],
     ]
     big = pltpu.VMEM((ROWS, HALF), F32)
-    ends = pltpu.VMEM((TM, PAIR, HALF), BF16)
+    ends = pltpu.VMEM((TM, PAIR, HALF), F32)
     narrow = pltpu.VMEM((ROWS, 128), F32)
     scratch = [
+        *[pltpu.VMEM(a.shape, a.dtype) for a in small],
         pltpu.VMEM((ROWS, D), BF16), pltpu.VMEM((ROWS, D), BF16),
         pltpu.VMEM((ROWS, D), BF16), pltpu.VMEM((ROWS, D), BF16),
         pltpu.VMEM((4, 4, 4, 32, ROWS), BF16), pltpu.VMEM((2, 16, HALF), BF16),
-        *weights, *weights,
+        *weights,
         pltpu.VMEM((6, PAIR, 128), F32), pltpu.VMEM((6, PAIR, 128), F32),
         narrow, narrow, narrow, narrow,
         big, big, big, big, big, big,
-        pltpu.VMEM((TM, 2, PAIR, 128), F32), pltpu.VMEM((TM, PAIR, HALF), F32), ends, ends, ends,
+        pltpu.VMEM((TM, 2, PAIR, 128), F32), ends, ends, ends, ends, pltpu.VMEM((TM, PAIR, HALF), BF16),
         pltpu.VMEM((PAIR, HALF), F32),
         pltpu.VMEM((2, 2, PAIR, 128), F32), pltpu.VMEM((2, 2, PAIR, 128), F32),
         pltpu.VMEM((3, PAIR, 128), F32), pltpu.VMEM((3, PAIR, 128), F32),
@@ -695,10 +795,10 @@
         *[pltpu.VMEM((4, 4, 4, 32, w), F32) for w in WIDTHS],
         *staged, *staged,
         pltpu.VMEM((16, HALF), F32), pltpu.VMEM((16, HALF), F32),
-        pltpu.SemaphoreType.DMA((18,)), pltpu.SemaphoreType.DMA((6 * AG_SEMS,)),
+        pltpu.SemaphoreType.DMA((18,)), pltpu.SemaphoreType.DMA((6 * AG_SEMS + 3,)),
         pltpu.SemaphoreType.DMA((9,)), pltpu.SemaphoreType.DMA((3 * RS_SEMS,)),
         pltpu.SemaphoreType.DMA((8,)), pltpu.SemaphoreType.DMA((8,)),
-        pltpu.SemaphoreType.DMA((2,)),
+        pltpu.SemaphoreType.DMA((2,)), pltpu.SemaphoreType.DMA((9,)),
         pltpu.SemaphoreType.DMA((8,)), pltpu.SemaphoreType.DMA((8,)),
         pltpu.SemaphoreType.DMA((2,)),
     ]
@@ -710,20 +810,27 @@
             jax.ShapeDtypeStruct(online_w.shape, F32),
             jax.ShapeDtypeStruct(reward.shape, F32),
         ),
-        in_specs=[hbm, hbm] + [vmem] * 9 + [smem] * 2,
+        in_specs=[hbm] * 11 + [smem] * 2,
         out_specs=(vmem, vmem),
         scratch_shapes=scratch,
         compiler_params=pltpu.CompilerParams(
-            collective_id=0, has_side_effects=True, vmem_limit_bytes=62 * 1024 * 1024
+            collective_id=0, has_side_effects=True, vmem_limit_bytes=VMEM_LIMIT * 1024 * 1024
         ),
     )(
         obs_feats.reshape(rows_b * span, width), next_feats.reshape(rows_b * span, width),
-        online_w, target_w, log_decay[None], step_scale, online_heads, target_heads,
-        reward, next_action_log_prob, resets, horizon, burn_in,
+        *small, horizon, burn_in,
     )
-    grad_w = grad * SCALE
-    new_target = (1.0 - POLYAK_RATE) * target_w + POLYAK_RATE * (online_w - STEP_SIZE * grad_w)
-    return grad_w, new_target, returns
+    return pl.pallas_call(
+        update,
+        name="target_update",
+        out_shape=(
+            jax.ShapeDtypeStruct(online_w.shape, F32),
+            jax.ShapeDtypeStruct(target_w.shape, F32),
+            jax.ShapeDtypeStruct(reward.shape, F32),
+        ),
+        in_specs=[vmem] * 4,
+        out_specs=(vmem, vmem, vmem),
+    )(grad, returns, online_w, target_w)
 
 
 def solution(mesh):

time: 106 us -> 99.7 us (0.941)
  Pallas kernels: 103 us -> 98.8 us
  other arithmetic: 1.64 us -> 0 us
  local copies, waits for them, and re-layouts: 1.24 us -> 0 us
    pallas_call x1, Pallas kernels: 103 us -> 97.1 us  [shards(): pl.pallas_call(kernel, name='critic_step', out_shape=(jax.ShapeDtypeStruc...]
    pallas_call x0 -> x1, Pallas kernels: none -> 1.77 us  [shards(): pl.pallas_call(update, name='target_update', out_shape=(jax.ShapeDtypeStr...]
    add x1 -> x0, other arithmetic: 1.64 us -> none  [shards(): (1.0 - POLYAK_RATE) * target_w]
    unnamed x7 -> x0, local copies, waits for them, and re-layouts: 1.24 us -> none
where the time goes in v3:
time: 99.7 us; the launch traced here: 99.5 us
  Pallas kernels  98.8 us (99%)
    pallas_call x1, Pallas kernels, shards(): pl.pallas_call(kernel, name='critic_step', out_shape=(jax.ShapeDtypeStruc...  97.1 us

profile of v3, /device:TPU:1, one launch (start us, length us, event | category | flops | bytes accessed | tf_op | source)
XLA Modules:
  0.0 99.5 jit_solution(12587069759522103312)
XLA Ops:
  0.6 97.1 %critic_step.1 = (f32[16,2048]{1,0:T(8,128)}, f32[4,64]{1,0:T(4,128)}) custom-call(bf16[256,2048]{1,0:T(8,128)(2,1)} %bitcast.3, bf16[256,2048]{1,0:T(8,128)(2,1)} %bitcast.4, f32[16,2048]{1,0:T(8,128)} %onw.1, f32[16,2048]{1,0:T(8,128)} %tgw.1, f32[1,2048]{1,0:T(1,128)} %bitcast.5, f32[4,64]{1,0:T(4,128)} %step_in.1, f32[2,2048]{1,0:T(2,128)} %onh_in.1, ...), custom_call_target="tpu_custom_call" | custom-call | tf_op jit(solution)/shard_map/critic_step/pallas_call | solution.py:806
  97.7 1.8 %target_update.1 = (f32[16,2048]{1,0:T(8,128)}, f32[16,2048]{1,0:T(8,128)}, f32[4,64]{1,0:T(4,128)}) custom-call(f32[16,2048]{1,0:T(8,128)} %get-tuple-element.5.grad, f32[4,64]{1,0:T(4,128)} %get-tuple-element.6.returns, f32[16,2048]{1,0:T(8,128)} %onw.1, f32[16,2048]{1,0:T(8,128)} %tgw.1), custom_call_target="tpu_custom_call" | custom-call | tf_op jit(solution)/shard_map/target_update/pallas_call | solution.py:823

commit v4 on v3

--- a/solution.py
+++ b/solution.py
@@ -31,8 +31,8 @@
 OFFSETS = (0, 256, 640)
 ORDERS = (("z", "x", "y"), ("y", "z", "x"), ("x", "y", "z"))
 PARTS = (0, 2, 1)
-AG_SEMS = 13
-RS_SEMS = 16
+AG_SEMS = 8
+RS_SEMS = 11
 LINES = (2, 3, 1, 0)
 
 
@@ -63,9 +63,9 @@
     rcv_h, rcv_w, rcv_b = (rh0, rh1, rh2), (rw0, rw1, rw2), (rb0, rb1, rb2)
     pending = []
 
-    def device(**moved):
+    def device(core=c, **moved):
         here = {**at, **moved}
-        return {"tm": here["y"] * 4 + here["x"], "batch": here["z"] * 2 + c}
+        return {"tm": here["y"] * 4 + here["x"], "batch": here["z"] * 2 + core}
 
     partner = {"tm": tm, "batch": z * 2 + other}
 
@@ -82,6 +82,8 @@
 
     barrier = pltpu.get_barrier_semaphore()
     peers = [partner] + [device(z=lax.rem(z + d, 4)) for d in range(1, 4)]
+    for a in "yxz":
+        peers += [device(core=other, **{a: lax.rem(at[a] + d, 4)}) for d in range(1, 4)]
     peers += [{"tm": lax.rem(tm + d, TM), "batch": batch} for d in range(1, TM)]
     for dev in peers:
         pl.semaphore_signal(barrier, inc=1, device_id=dev, device_id_type=MESH)
@@ -164,8 +166,8 @@
     def turned(p, i, d):
         return lax.rem(at[ORDERS[p][i]] + d, 4)
 
-    def toward(p, i, d):
-        return device(**{ORDERS[p][i]: turned(p, i, d)})
+    def toward(p, i, d, core=c):
+        return device(core=core, **{ORDERS[p][i]: turned(p, i, d)})
 
     FULL = pl.ds(0, 4)
 
@@ -178,7 +180,7 @@
         return remote(ref, ref, ag_ss.at[n * 3 + k], ag_rs.at[n * AG_SEMS + j], dev)
 
     def ag_end(m, p, l):
-        return 12 + l if (m, p) == (1, 2) else 12
+        return 7 + l if (m, p) == (1, 2) else 7
 
     def ag_send(m, p, k, j, where, dev):
         ag_copy(m, p, k, j, where, dev).start()
@@ -194,56 +196,53 @@
         return place(p, half_of(h), second, last)
 
     def ag_one(m, p):
+        dst = wb[m][p].at[y, x, z, own_rows, :]
+        sem, n = ag_ss.at[(m * 3 + p) * 3], (m * 3 + p) * AG_SEMS
         for d in (2, 1, 3):
-            ag_send(m, p, 0, 0, (y, x, z), toward(p, 0, d))
+            remote(dst, dst, sem, ag_rs.at[n], toward(p, 0, d)).start()
+            src = wst.at[m, :, cols_of(p, m)]
+            remote(src, dst, sem, ag_rs.at[n], toward(p, 0, d, other)).start()
 
     def ag_one_in(m, p):
         ag_wait(m, p, 0, (0, 0, pl.ds(0, 3)))
 
-    def ag_two(m, p):
+    def ag_own(m, p, k):
         for d in (1, 3, 2):
             where = place(p, turned(p, 0, d), turned(p, 1, 0), turned(p, 2, 0))
-            ag_send(m, p, 1, 1, where, toward(p, 1, 1))
-            ag_send(m, p, 1, 2, where, toward(p, 1, 3))
-
-    def ag_three_own(m, p):
-        for d in (1, 3, 2):
-            where = place(p, turned(p, 0, d), turned(p, 1, 0), turned(p, 2, 0))
-            ag_send(m, p, 2, 4, where, toward(p, 2, 1))
-            ag_send(m, p, 2, 5, where, toward(p, 2, 3))
+            ag_send(m, p, k, 2 * k - 1, where, toward(p, k, 1))
+            ag_send(m, p, k, 2 * k - 1, where, toward(p, k, 3))
 
     def ag_early(m, p):
         for k in (1, 2):
-            ag_send(m, p, k, 3 * k - 2, (y, x, z), toward(p, k, 1))
-            ag_send(m, p, k, 3 * k - 1, (y, x, z), toward(p, k, 3))
+            ag_send(m, p, k, 2 * k - 1, (y, x, z), toward(p, k, 1))
+            ag_send(m, p, k, 2 * k - 1, (y, x, z), toward(p, k, 3))
 
     def ag_two_forward(m, p):
         q3 = turned(p, 2, 0)
-        ag_wait(m, p, 1, line(p, turned(p, 1, 3), q3))
-        ag_send(m, p, 1, 3, line(p, turned(p, 1, 3), q3, 0), toward(p, 1, 1))
-        ag_wait(m, p, 2, line(p, turned(p, 1, 1), q3))
-        ag_send(m, p, 1, 3, line(p, turned(p, 1, 1), q3, 1), toward(p, 1, 3))
+        ag_wait(m, p, 1, (0, pl.ds(0, 2)))
+        ag_send(m, p, 1, 2, line(p, turned(p, 1, 3), q3, 0), toward(p, 1, 1))
+        ag_send(m, p, 1, 2, line(p, turned(p, 1, 1), q3, 1), toward(p, 1, 3))
 
     def ag_two_last(m, p):
-        ag_wait(m, p, 3, line(p, turned(p, 1, 2), turned(p, 2, 0)))
+        ag_wait(m, p, 2, line(p, turned(p, 1, 2), turned(p, 2, 0)))
 
     def ag_three(m, p, l):
         own = line(p, turned(p, 1, l), turned(p, 2, 0))
-        ag_send(m, p, 2, 4 + 2 * l, own, toward(p, 2, 1))
-        ag_send(m, p, 2, 5 + 2 * l, own, toward(p, 2, 3))
+        ag_send(m, p, 2, 3 + l, own, toward(p, 2, 1))
+        ag_send(m, p, 2, 3 + l, own, toward(p, 2, 3))
 
     def ag_three_forward(m, p, l):
         second = turned(p, 1, l)
-        ag_wait(m, p, 4 + 2 * l, line(p, second, turned(p, 2, 3)))
-        ag_send(m, p, 2, ag_end(m, p, l), line(p, second, turned(p, 2, 3), 0), toward(p, 2, 1))
-        ag_wait(m, p, 5 + 2 * l, line(p, second, turned(p, 2, 1)))
-        ag_send(m, p, 2, ag_end(m, p, l), line(p, second, turned(p, 2, 1), 1), toward(p, 2, 3))
+        ag_wait(m, p, 3 + l, (0, pl.ds(0, 2)))
+        end = ag_end(m, p, l)
+        ag_send(m, p, 2, end, line(p, second, turned(p, 2, 3), 0), toward(p, 2, 1))
+        ag_send(m, p, 2, end, line(p, second, turned(p, 2, 1), 1), toward(p, 2, 3))
 
     def ag_three_last(m, p):
-        ag_wait(m, p, 12, place(p, FULL, FULL, turned(p, 2, 2)))
+        ag_wait(m, p, 7, place(p, FULL, FULL, turned(p, 2, 2)))
 
     def ag_line_last(l):
-        ag_wait(1, 2, 12 + l, line(2, turned(2, 1, l), turned(2, 2, 2)))
+        ag_wait(1, 2, 7 + l, line(2, turned(2, 1, l), turned(2, 2, 2)))
 
     def wide(v, w=HALF):
         return jnp.concatenate([v] * (w // 128), axis=1)
@@ -326,7 +325,7 @@
             return st
 
         last = lax.fori_loop(0, T // 4, body, jnp.zeros((PAIR, width(m, p)), F32))
-        ends[tm, :, cols] = last
+        ends[tm, :, cols] = last.astype(BF16)
 
     def ends_copy(n, ends, p, slots, dev):
         cols = pl.ds(0, HALF) if p is None else cols_of(p)
@@ -413,21 +412,22 @@
         return [(q_s[slot, k] + q_r[slot, k]) * (H ** (-0.5)) for k in range(2)]
 
     for m in range(2):
+        for p in range(3):
+            ag_one(m, p)
+    for m in range(2):
         w_half_in(m)
         for p in range(3):
-            ag_one(m, p)
-        for p in range(3):
             ag_early(m, p)
     for p in range(3):
         ag_one_in(0, p)
-        ag_two(0, p)
-    for p in range(3):
-        ag_three_own(0, p)
+        ag_own(0, p, 1)
+    for p in range(3):
+        ag_own(0, p, 2)
     def clear(j, _):
         @pl.when(j > tm)
         def _():
-            ends_t[j] = jnp.zeros((PAIR, HALF), F32)
-            ends_o[j] = jnp.zeros((PAIR, HALF), F32)
+            ends_t[j] = jnp.zeros((PAIR, HALF), BF16)
+            ends_o[j] = jnp.zeros((PAIR, HALF), BF16)
 
         @pl.when(j < tm)
         def _():
@@ -467,7 +467,7 @@
     lax.fori_loop(0, T, factors, jnp.ones((PAIR, HALF), F32))
     for p in range(3):
         ag_one_in(1, p)
-        ag_two(1, p)
+        ag_own(1, p, 1)
     for p in range(3):
         ag_two_forward(0, p)
         ag_three(0, p, 3)
@@ -488,7 +488,7 @@
             ag_three_forward(0, p, l)
     for p in range(3):
         ag_two_forward(1, p)
-        ag_three_own(1, p)
+        ag_own(1, p, 2)
     def tails(i, prod):
         t = T - 1 - i
         tp[at_t(t), :] = prod
@@ -593,27 +593,23 @@
     spread_lanes(bc0, weight * (oq[0] - total) * (H ** (-0.5)))
     spread_lanes(bc1, weight * (oq[1] - total) * (H ** (-0.5)))
 
-    for p in PARTS:
-        cols, w = cols_of(p), WIDTHS[p]
-        hcols = pl.ds(pl.multiple_of(c * HALF + OFFSETS[p], 128), w)
-        h0 = jnp.broadcast_to(onh[0:1, hcols], (PAIR, w))
-        h1 = jnp.broadcast_to(onh[1:2, hcols], (PAIR, w))
-
-        def back(i, adj, cols=cols, w=w, h0=h0, h1=h1):
-            for k in range(4):
-                rows = at_t(T - 1 - (i * 4 + k))
-                dh = wide(bc0[rows, :], w) * h0 + wide(bc1[rows, :], w) * h1
-                adj = dh * vo[rows, cols] + adj
-                vo[rows, cols] = adj
-                adj = cc[rows, cols] * adj
-            return adj
-
-        leaving = lax.fori_loop(0, T // 4, back, jnp.zeros((PAIR, w), F32))
-        lv[tm, :, cols] = leaving.astype(BF16)
-        prefix_send(5 + p, lv, p, False)
+    h0 = jnp.broadcast_to(onh[0:1, mine], (PAIR, HALF))
+    h1 = jnp.broadcast_to(onh[1:2, mine], (PAIR, HALF))
+
+    def back(i, adj):
+        for k in range(4):
+            rows = at_t(T - 1 - (i * 4 + k))
+            dh = wide(bc0[rows, :]) * h0 + wide(bc1[rows, :]) * h1
+            adj = dh * vo[rows, :] + adj
+            vo[rows, :] = adj
+            adj = cc[rows, :] * adj
+        return adj
+
+    leaving = lax.fori_loop(0, T // 4, back, jnp.zeros((PAIR, HALF), F32))
+    lv[tm] = leaving.astype(BF16)
+    prefix_send(5, lv, None, False)
 
     def finish(p):
-        prefix_take(5 + p, lv, p, False)
         cols = cols_of(p)
         incoming = carry[:, cols]
         both = jnp.concatenate([incoming, incoming], axis=0)
@@ -637,10 +633,10 @@
         return remote(src, dst, rs_ss.at[p * 3 + k], rs_rs.at[p * RS_SEMS + j], dev)
 
     def rs_half(p, s, h, dev):
-        return rs_copy(p, 0, 2 * s + h, snd_h[p].at[s, h], rcv_h[p].at[s, h], dev)
+        return rs_copy(p, 0, s, snd_h[p].at[s, h], rcv_h[p].at[s, h], dev)
 
     def rs_whole(p, s, h, dev):
-        return rs_copy(p, 1, 10 + s, snd_w[p].at[s, h], rcv_w[p].at[s, h], dev)
+        return rs_copy(p, 1, 5 + s, snd_w[p].at[s, h], rcv_w[p].at[s, h], dev)
 
     def rs_drain(p):
         for k, (src, dst) in enumerate(
@@ -661,33 +657,40 @@
             snd_h[p][s, h] = gg[p][rs_ref(p, s, 2, h)].astype(BF16)
             rs_half(p, s, h, toward(p, rs_axis(s), d)).start()
 
+    def rs_arrived(p, s):
+        rs_copy(p, 0, s, snd_h[p].at[s], rcv_h[p].at[s], partner).wait_recv()
+
     def rs_neighbour(p, s, h):
         d = (3, 1)[h]
-        rs_half(p, s, h, partner).wait_recv()
         with_recv = gg[p][rs_ref(p, s, d, h)] + rcv_h[p][s, h].astype(F32)
         snd_w[p][s, h, pl.ds(2 * h, 2)] = with_recv.astype(BF16)
         snd_w[p][s, h, pl.ds(2 - 2 * h, 2)] = gg[p][rs_ref(p, s, d, 1 - h)].astype(BF16)
         rs_whole(p, s, h, toward(p, rs_axis(s), d)).start()
 
+    def rs_neighbours(p, s):
+        rs_arrived(p, s)
+        rs_neighbour(p, s, 0)
+        rs_neighbour(p, s, 1)
+
     def rs_sum(p, s):
-        rs_copy(p, 1, 10 + s, snd_w[p].at[s], rcv_w[p].at[s], partner).wait_recv()
+        rs_copy(p, 1, 5 + s, snd_w[p].at[s], rcv_w[p].at[s], partner).wait_recv()
         own = rs_ref(p, s, 0)
         both = rcv_w[p][s, 0].astype(F32) + rcv_w[p][s, 1].astype(F32)
         gg[p][own] = gg[p][own] + both
 
     def rs_one(p):
         for d in (2, 1, 3):
-            block = gg[p][place(p, turned(p, 0, d), turned(p, 1, 0), turned(p, 2, 0))]
-            snd_b[p][d - 1] = block.astype(BF16)
-            rs_copy(p, 2, 15, snd_b[p].at[d - 1], rcv_b[p].at[d - 1], toward(p, 0, d)).start()
-
-    def rs_one_sum(p):
-        rs_copy(p, 2, 15, snd_b[p], rcv_b[p], partner).wait_recv()
-        v = gg[p][y, x, z]
-        for d in range(3):
-            v = v + rcv_b[p][d].astype(F32)
-        gg[p][y, x, z] = v
-
+            where = place(p, turned(p, 0, d), turned(p, 1, 0), turned(p, 2, 0))
+            for core in range(2):
+                block = gg[p][(*where, pl.ds(16 * core, 16))]
+                snd_b[p][core, d - 1] = block.astype(BF16)
+                rs_copy(
+                    p, 2, 10, snd_b[p].at[core, d - 1], rcv_b[p].at[c, d - 1],
+                    toward(p, 0, d, core),
+                ).start()
+        gx_s[:, cols_of(p)] = gg[p][y, x, z, other_rows, :]
+
+    prefix_take(5, lv, None, False)
     for p in PARTS:
         finish(p)
         gradient(p, LINES[0])
@@ -696,57 +699,57 @@
         gradient(p, LINES[1])
         rs_opposite(p, LINES[1])
     for p in PARTS:
-        rs_neighbour(p, LINES[0], 0)
-        rs_neighbour(p, LINES[0], 1)
+        rs_neighbours(p, LINES[0])
         gradient(p, LINES[2])
         rs_opposite(p, LINES[2])
     for p in PARTS:
-        rs_neighbour(p, LINES[1], 0)
-        rs_neighbour(p, LINES[1], 1)
+        rs_neighbours(p, LINES[1])
         gradient(p, LINES[3])
         rs_opposite(p, LINES[3])
     for p in PARTS:
         rs_sum(p, LINES[0])
         rs_opposite(p, 4)
     for p in PARTS:
-        rs_neighbour(p, LINES[2], 0)
-        rs_neighbour(p, LINES[2], 1)
+        rs_neighbours(p, LINES[2])
     for p in PARTS:
         rs_sum(p, LINES[1])
+        rs_arrived(p, 4)
         rs_neighbour(p, 4, 0)
     for p in PARTS:
-        rs_neighbour(p, LINES[3], 0)
-        rs_neighbour(p, LINES[3], 1)
+        rs_neighbours(p, LINES[3])
     for p in PARTS:
         rs_sum(p, LINES[2])
         rs_neighbour(p, 4, 1)
+    prefix_drain(1, ends_t, None, True)
+    for p in range(3):
+        prefix_drain(2 + p, ends_o, p, True)
+        ag_drain(0, p)
+        ag_drain(1, p)
+    prefix_drain(5, lv, None, False)
+    remote(wst, wst, d2d_ss.at[0], d2d_rs.at[0], partner).wait_send()
+    sums.wait_send()
+    for copy in pending:
+        copy.wait_send()
+    pending.clear()
     for p in PARTS:
         rs_sum(p, LINES[3])
     for p in PARTS:
         rs_sum(p, 4)
         rs_one(p)
-    for p in PARTS:
-        rs_one_sum(p)
-
-    for p in range(3):
-        gx_s[:, cols_of(p)] = gg[p][y, x, z, other_rows, :]
     send(gx_s, gx_r, d2d_ss.at[7], d2d_rs.at[7], partner)
-    for p in range(3):
-        cols = pl.ds(pl.multiple_of(c * HALF + OFFSETS[p], 128), WIDTHS[p])
-        gw[:, cols] = gg[p][y, x, z, own_rows, :]
     remote(gx_s, gx_r, d2d_ss.at[7], d2d_rs.at[7], partner).wait_recv()
-    gw[:, theirs] = gx_r[...]
-
-    prefix_drain(1, ends_t, None, True)
-    for p in range(3):
-        prefix_drain(2 + p, ends_o, p, True)
-        prefix_drain(5 + p, lv, p, False)
-    for p in range(3):
-        ag_drain(0, p)
-        ag_drain(1, p)
+    for p in range(3):
+        rs_copy(p, 2, 10, snd_b[p], rcv_b[p], partner).wait_recv()
+        for core, v in (
+            (c, gg[p][y, x, z, own_rows, :]), (other, gx_r[:, cols_of(p)]),
+        ):
+            for d in range(3):
+                v = v + rcv_b[p][core, d].astype(F32)
+            cols = pl.ds(pl.multiple_of(core * HALF + OFFSETS[p], 128), WIDTHS[p])
+            gw[:, cols] = v
+
+    for p in range(3):
         rs_drain(p)
-    remote(wst, wst, d2d_ss.at[0], d2d_rs.at[0], partner).wait_send()
-    sums.wait_send()
     for copy in pending:
         copy.wait_send()
 
@@ -773,10 +776,11 @@
     staged = [
         *[pltpu.VMEM((5, 2, 2, 32, w), BF16) for w in WIDTHS],
         *[pltpu.VMEM((5, 2, 4, 32, w), BF16) for w in WIDTHS],
-        *[pltpu.VMEM((3, 32, w), BF16) for w in WIDTHS],
+        *[pltpu.VMEM((2, 3, 16, w), BF16) for w in WIDTHS],
     ]
     big = pltpu.VMEM((ROWS, HALF), F32)
-    ends = pltpu.VMEM((TM, PAIR, HALF), F32)
+    table = pltpu.VMEM((TM, PAIR, HALF), F32)
+    ends = pltpu.VMEM((TM, PAIR, HALF), BF16)
     narrow = pltpu.VMEM((ROWS, 128), F32)
     scratch = [
         *[pltpu.VMEM(a.shape, a.dtype) for a in small],
@@ -787,7 +791,7 @@
         pltpu.VMEM((6, PAIR, 128), F32), pltpu.VMEM((6, PAIR, 128), F32),
         narrow, narrow, narrow, narrow,
         big, big, big, big, big, big,
-        pltpu.VMEM((TM, 2, PAIR, 128), F32), ends, ends, ends, ends, pltpu.VMEM((TM, PAIR, HALF), BF16),
+        pltpu.VMEM((TM, 2, PAIR, 128), F32), table, table, ends, ends, ends,
         pltpu.VMEM((PAIR, HALF), F32),
         pltpu.VMEM((2, 2, PAIR, 128), F32), pltpu.VMEM((2, 2, PAIR, 128), F32),
         pltpu.VMEM((3, PAIR, 128), F32), pltpu.VMEM((3, PAIR, 128), F32),
@@ -797,7 +801,7 @@
         pltpu.VMEM((16, HALF), F32), pltpu.VMEM((16, HALF), F32),
         pltpu.SemaphoreType.DMA((18,)), pltpu.SemaphoreType.DMA((6 * AG_SEMS + 3,)),
         pltpu.SemaphoreType.DMA((9,)), pltpu.SemaphoreType.DMA((3 * RS_SEMS,)),
-        pltpu.SemaphoreType.DMA((8,)), pltpu.SemaphoreType.DMA((8,)),
+        pltpu.SemaphoreType.DMA((6,)), pltpu.SemaphoreType.DMA((6,)),
         pltpu.SemaphoreType.DMA((2,)), pltpu.SemaphoreType.DMA((9,)),
         pltpu.SemaphoreType.DMA((8,)), pltpu.SemaphoreType.DMA((8,)),
         pltpu.SemaphoreType.DMA((2,)),

time: 99.7 us -> 96.9 us (0.972)
  Pallas kernels: 98.8 us -> 96.1 us
    pallas_call x1, Pallas kernels: 97.1 us -> 94.4 us  [shards(): pl.pallas_call(kernel, name='critic_step', out_shape=(jax.ShapeDtypeStruc...]
where the time goes in v4:
time: 96.9 us; the launch traced here: 96.8 us
  Pallas kernels  96.1 us (99%)
    pallas_call x1, Pallas kernels, shards(): pl.pallas_call(kernel, name='critic_step', out_shape=(jax.ShapeDtypeStruc...  94.4 us

profile of v4, /device:TPU:1, one launch (start us, length us, event | category | flops | bytes accessed | tf_op | source)
XLA Modules:
  0.0 96.8 jit_solution(6523386303453374121)
XLA Ops:
  0.6 94.4 %critic_step.1 = (f32[16,2048]{1,0:T(8,128)}, f32[4,64]{1,0:T(4,128)}) custom-call(bf16[256,2048]{1,0:T(8,128)(2,1)} %bitcast.3, bf16[256,2048]{1,0:T(8,128)(2,1)} %bitcast.4, f32[16,2048]{1,0:T(8,128)} %onw.1, f32[16,2048]{1,0:T(8,128)} %tgw.1, f32[1,2048]{1,0:T(1,128)} %bitcast.5, f32[4,64]{1,0:T(4,128)} %step_in.1, f32[2,2048]{1,0:T(2,128)} %onh_in.1, ...), custom_call_target="tpu_custom_call" | custom-call | tf_op jit(solution)/shard_map/critic_step/pallas_call | solution.py:810
  95.0 1.8 %target_update.1 = (f32[16,2048]{1,0:T(8,128)}, f32[16,2048]{1,0:T(8,128)}, f32[4,64]{1,0:T(4,128)}) custom-call(f32[16,2048]{1,0:T(8,128)} %get-tuple-element.5.grad, f32[4,64]{1,0:T(4,128)} %get-tuple-element.6.returns, f32[16,2048]{1,0:T(8,128)} %onw.1, f32[16,2048]{1,0:T(8,128)} %tgw.1), custom_call_target="tpu_custom_call" | custom-call | tf_op jit(solution)/shard_map/target_update/pallas_call | solution.py:827

commit v5 on v4

--- a/solution.py
+++ b/solution.py
@@ -31,6 +31,7 @@
 OFFSETS = (0, 256, 640)
 ORDERS = (("z", "x", "y"), ("y", "z", "x"), ("x", "y", "z"))
 PARTS = (0, 2, 1)
+RS_PARTS = (2, 1, 0)
 AG_SEMS = 8
 RS_SEMS = 11
 LINES = (2, 3, 1, 0)
@@ -44,7 +45,7 @@
     wt0, wt1, wt2, wo0, wo1, wo2,
     pk_m, pk_i, bc0, bc1, qa0, qa1, cc, ss, pf, tp, vt, vo,
     sf, dfor, dback, ends_t, ends_o, lv, carry,
-    q_s, q_r, nb_s, nb_r, du,
+    q_s, q_r, q_n, nb_s, nb_r, du,
     g0, g1, g2,
     sh0, sh1, sh2, sw0, sw1, sw2, sb0, sb1, sb2,
     rh0, rh1, rh2, rw0, rw1, rw2, rb0, rb1, rb2,
@@ -80,14 +81,6 @@
         copy.start()
         pending.append(copy)
 
-    barrier = pltpu.get_barrier_semaphore()
-    peers = [partner] + [device(z=lax.rem(z + d, 4)) for d in range(1, 4)]
-    for a in "yxz":
-        peers += [device(core=other, **{a: lax.rem(at[a] + d, 4)}) for d in range(1, 4)]
-    peers += [{"tm": lax.rem(tm + d, TM), "batch": batch} for d in range(1, TM)]
-    for dev in peers:
-        pl.semaphore_signal(barrier, inc=1, device_id=dev, device_id_type=MESH)
-
     own_half = pl.ds(pl.multiple_of(c * 256, 256), 256)
     other_half = pl.ds(pl.multiple_of(other * 256, 256), 256)
     loads = [
@@ -103,6 +96,14 @@
     ]
     for copy in loads + local:
         copy.start()
+    barrier = pltpu.get_barrier_semaphore()
+    peers = [partner] + [device(z=lax.rem(z + d, 4)) for d in range(1, 4)]
+    for a in "yxz":
+        peers += [device(core=other, **{a: lax.rem(at[a] + d, 4)}) for d in range(1, 4)]
+    peers += [{"tm": lax.rem(tm + d, TM), "batch": batch} for d in range(1, TM)]
+    peers += [{"tm": lax.rem(tm + d, TM), "batch": z * 2 + other} for d in (1, TM - 1)]
+    for dev in peers:
+        pl.semaphore_signal(barrier, inc=1, device_id=dev, device_id_type=MESH)
     for copy in loads:
         copy.wait()
 
@@ -177,10 +178,10 @@
     def ag_copy(m, p, k, j, where, dev):
         ref = wb[m][p].at[where]
         n = m * 3 + p
-        return remote(ref, ref, ag_ss.at[n * 3 + k], ag_rs.at[n * AG_SEMS + j], dev)
+        return remote(ref, ref, ag_ss.at[n * 3 + k], ag_rs.at[n * AG_SEMS + 3 * m + j], dev)
 
     def ag_end(m, p, l):
-        return 7 + l if (m, p) == (1, 2) else 7
+        return 7 + l if p == 2 else 7
 
     def ag_send(m, p, k, j, where, dev):
         ag_copy(m, p, k, j, where, dev).start()
@@ -197,7 +198,7 @@
 
     def ag_one(m, p):
         dst = wb[m][p].at[y, x, z, own_rows, :]
-        sem, n = ag_ss.at[(m * 3 + p) * 3], (m * 3 + p) * AG_SEMS
+        sem, n = ag_ss.at[(m * 3 + p) * 3], (m * 3 + p) * AG_SEMS + 3 * m
         for d in (2, 1, 3):
             remote(dst, dst, sem, ag_rs.at[n], toward(p, 0, d)).start()
             src = wst.at[m, :, cols_of(p, m)]
@@ -241,8 +242,8 @@
     def ag_three_last(m, p):
         ag_wait(m, p, 7, place(p, FULL, FULL, turned(p, 2, 2)))
 
-    def ag_line_last(l):
-        ag_wait(1, 2, 7 + l, line(2, turned(2, 1, l), turned(2, 2, 2)))
+    def ag_line_last(m, l):
+        ag_wait(m, 2, 7 + l, line(2, turned(2, 1, l), turned(2, 2, 2)))
 
     def wide(v, w=HALF):
         return jnp.concatenate([v] * (w // 128), axis=1)
@@ -282,34 +283,26 @@
 
         lax.fori_loop(lo, hi, body, 0)
 
-    def project(m, p, xp, v):
+    def project_planes(m, p, planes, fresh):
+        xp, v = (xp_n, vt) if m == 0 else (xp_o, vo)
+        cols, w = cols_of(p, m), width(m, p)
+        axis = 1 if p == 2 else 2
+        qs = [turned(p, axis, d) for d in planes]
+
         def tile(i, _):
             rows = pl.ds(pl.multiple_of(i * 256, 256), 256)
-            w = wb[m][p][...].reshape(D, width(m, p))
-            acc = jnp.dot(xp[rows, :], w, preferred_element_type=F32)
-            v[rows, cols_of(p, m)] = acc * SCALE
-            return 0
-
-        lax.fori_loop(0, ROWS // 256, tile, 0)
-
-    def project_planes(p, planes, fresh):
-        axis = 1 if p == 2 else 2
-        qs = [turned(p, axis, d) for d in planes]
-
-        def tile(i, _):
-            rows = pl.ds(pl.multiple_of(i * 256, 256), 256)
-            acc = None if fresh else vo[rows, cols_of(p)]
+            acc = None if fresh else v[rows, cols]
             for q in qs:
                 where = place(p, FULL, q, FULL) if p == 2 else place(p, FULL, FULL, q)
-                w = wb[1][p][where].reshape(512, WIDTHS[p])
+                rhs = wb[m][p][where].reshape(512, w)
                 if p == 1:
                     starts = [pl.multiple_of((k * 4 + q) * 128, 128) for k in range(4)]
-                    lhs = jnp.concatenate([xp_o[rows, pl.ds(k, 128)] for k in starts], axis=1)
+                    lhs = jnp.concatenate([xp[rows, pl.ds(k, 128)] for k in starts], axis=1)
                 else:
-                    lhs = xp_o[rows, pl.ds(pl.multiple_of(q * 512, 512), 512)]
-                v = jnp.dot(lhs, w, preferred_element_type=F32) * SCALE
-                acc = v if acc is None else acc + v
-            vo[rows, cols_of(p)] = acc
+                    lhs = xp[rows, pl.ds(pl.multiple_of(q * 512, 512), 512)]
+                part = jnp.dot(lhs, rhs, preferred_element_type=F32) * SCALE
+                acc = part if acc is None else acc + part
+            v[rows, cols] = acc
             return 0
 
         lax.fori_loop(0, ROWS // 256, tile, 0)
@@ -318,10 +311,15 @@
         cols = cols_of(p, m)
 
         def body(i, st):
-            for k in range(4):
-                rows = at_t(i * 4 + k)
-                st = cc[rows, cols] * st + ss[rows, cols] * v[rows, cols]
-                v[rows, cols] = st
+            steps = [at_t(i * 4 + k) for k in range(4)]
+            added = [ss[rows, cols] * v[rows, cols] for rows in steps]
+            kept = [cc[rows, cols] for rows in steps]
+            states = []
+            for f, u in zip(kept, added):
+                st = f * st + u
+                states.append(st)
+            for rows, state in zip(steps, states):
+                v[rows, cols] = state
             return st
 
         last = lax.fori_loop(0, T // 4, body, jnp.zeros((PAIR, width(m, p)), F32))
@@ -375,16 +373,19 @@
             return out
 
         def body(i, _):
-            for k in range(8):
-                rows = at_t(i * 8 + k)
-                st = v[rows, cols] + pf[rows, cols] * start
+            steps = [at_t(i * 8 + k) for k in range(8)]
+            states = [v[rows, cols] + pf[rows, cols] * start for rows in steps]
+            before = None if fresh else [(qa0[rows, :], qa1[rows, :]) for rows in steps]
+            out = []
+            for st in states:
                 sig = 1.0 / (1.0 + jnp.exp(-st))
                 act = st * sig
+                out.append((fold(act * h0), fold(act * h1), sig + act * (1.0 - sig)))
+            for k, (rows, (f0, f1, rise)) in enumerate(zip(steps, out)):
+                qa0[rows, :] = f0 if fresh else before[k][0] + f0
+                qa1[rows, :] = f1 if fresh else before[k][1] + f1
                 if slope:
-                    v[rows, cols] = sig + act * (1.0 - sig)
-                f0, f1 = fold(act * h0), fold(act * h1)
-                qa0[rows, :] = f0 if fresh else qa0[rows, :] + f0
-                qa1[rows, :] = f1 if fresh else qa1[rows, :] + f1
+                    v[rows, cols] = rise
             return 0
 
         lax.fori_loop(0, T // 8, body, 0)
@@ -409,7 +410,7 @@
         remote(
             q_s.at[slot], q_r.at[slot], d2d_ss.at[5 + slot], d2d_rs.at[5 + slot], partner
         ).wait_recv()
-        return [(q_s[slot, k] + q_r[slot, k]) * (H ** (-0.5)) for k in range(2)]
+        return [q_s[slot, k] + q_r[slot, k] for k in range(2)]
 
     for m in range(2):
         for p in range(3):
@@ -451,6 +452,12 @@
         dev = {"tm": lax.rem(tm + d, TM), "batch": batch}
         remote(sf.at[tm], sf.at[tm], pre_ss.at[0], pre_rs.at[0], dev).start()
 
+    nb_s[0] = rew8
+    nb_s[1] = logp8
+    nb_s[2] = keep8
+    earlier = lax.rem(tm + TM - 1, TM)
+    before = {"tm": earlier, "batch": batch}
+    send(nb_s, nb_r, nb_sem.at[0], nb_sem.at[1], before)
     spread_lanes(bc0, step8)
     spread_lanes(bc1, keep8)
     ld8 = jnp.broadcast_to(ld[:, mine], (PAIR, HALF))
@@ -499,6 +506,8 @@
         ag_three_forward(0, p, 2)
         ag_three(1, p, 3)
         ag_three(1, p, 1)
+    for p in (0, 1):
+        project_planes(0, p, (0, 1, 3), True)
     for p in range(3):
         ag_two_last(1, p)
         ag_three(1, p, 2)
@@ -516,64 +525,72 @@
     lax.fori_loop(0, TM, block_decay, 0)
     for p in range(3):
         ag_three_forward(1, p, 0)
-    for p in PARTS[:2]:
-        ag_three_last(0, p)
-        project(0, p, xp_n, vt)
-        scan(0, vt, p, ends_t)
-    for p in range(3):
-        ag_three_forward(1, p, 3)
-    for p in PARTS[2:]:
-        ag_three_last(0, p)
-        project(0, p, xp_n, vt)
+    for p in (0, 1, 2):
+        if p == 2:
+            for l in range(4):
+                ag_line_last(0, l)
+            project_planes(0, p, (0, 1, 3, 2), True)
+        else:
+            ag_three_last(0, p)
+            project_planes(0, p, (2,), False)
         scan(0, vt, p, ends_t)
     prefix_send(1, ends_t, None, True)
     for p in range(3):
+        ag_three_forward(1, p, 3)
+    for p in range(3):
         ag_three_forward(1, p, 1)
+    for p in (0, 1):
+        project_planes(1, p, (0,), True)
     for p in range(3):
         ag_three_forward(1, p, 2)
     for p in (0, 1):
-        project_planes(p, (0, 1, 3), True)
+        project_planes(1, p, (1, 3), False)
     for l in (0, 3, 1):
-        ag_line_last(l)
-    project_planes(2, (0, 1, 3), True)
+        ag_line_last(1, l)
+    project_planes(1, 2, (0, 1, 3), True)
     ag_three_last(1, 0)
-    project_planes(0, (2,), False)
+    project_planes(1, 0, (2,), False)
     scan(1, vo, PARTS[0], ends_o)
     prefix_send(2 + PARTS[0], ends_o, PARTS[0], True)
-    ag_line_last(2)
-    project_planes(2, (2,), False)
+    ag_line_last(1, 2)
+    project_planes(1, 2, (2,), False)
     scan(1, vo, PARTS[1], ends_o)
     prefix_send(2 + PARTS[1], ends_o, PARTS[1], True)
     ag_three_last(1, 1)
-    project_planes(1, (2,), False)
+    project_planes(1, 1, (2,), False)
     scan(1, vo, PARTS[2], ends_o)
     prefix_send(2 + PARTS[2], ends_o, PARTS[2], True)
     prefix_take(1, ends_t, None, True)
     for p in PARTS:
         quality(0, vt, tgh, p, p == PARTS[0], False)
     quality_send(0)
+    for core in range(2):
+        dev = {"tm": earlier, "batch": z * 2 + core}
+        remote(q_s.at[0], q_n.at[c], nb_sem.at[2], nb_sem.at[3], dev).start()
     prefix_take(2 + PARTS[0], ends_o, PARTS[0], True)
     quality(1, vo, onh, PARTS[0], True, True)
 
-    tq = quality_sum(0)
-    value8 = jnp.minimum(tq[0], tq[1]) - ENTROPY_COEFF * logp8
-    nb_s[0] = rew8
-    nb_s[1] = value8
-    nb_s[2] = keep8
-    before = {"tm": lax.rem(tm + TM - 1, TM), "batch": batch}
-    send(nb_s, nb_r, nb_sem.at[0], nb_sem.at[1], before)
     for p in PARTS[1:]:
         prefix_take(2 + p, ends_o, p, True)
         quality(1, vo, onh, p, False, True)
     quality_send(1)
+    def value_of(products, log_prob):
+        tq = [v * (H ** (-0.5)) for v in products]
+        return jnp.minimum(tq[0], tq[1]) - ENTROPY_COEFF * log_prob
+
+    value8 = value_of(quality_sum(0), logp8)
     remote(nb_s, nb_r, nb_sem.at[0], nb_sem.at[1], before).wait_recv()
+    later_q = remote(q_n, q_n, nb_sem.at[2], nb_sem.at[3], before)
+    later_q.wait_recv()
+    later_value = value_of([q_n[0, k] + q_n[1, k] for k in range(2)], nb_r[1])
     inside = (lane8 >= T) & (lane8 < T + NMAX) & (tm < TM - 1)
 
-    def extended(own, slot):
-        later = jnp.where(inside, pltpu.roll(nb_r[slot], T, 1), 0.0)
+    def extended(own, later):
+        later = jnp.where(inside, pltpu.roll(later, T, 1), 0.0)
         return jnp.where(lane8 < T, own, later)
 
-    ext_r, ext_v, ext_k = extended(rew8, 0), extended(value8, 1), extended(keep8, 2)
+    ext_r, ext_v = extended(rew8, nb_r[0]), extended(value8, later_value)
+    ext_k = extended(keep8, nb_r[2])
 
     def shifted(v, n):
         return v if n == 0 else pltpu.roll(v, 128 - n, 1)
@@ -590,22 +607,24 @@
     weight = jnp.where((lane8 + tm * T).astype(F32) >= burn8, 1.0, 0.0)
 
     oq = quality_sum(1)
-    spread_lanes(bc0, weight * (oq[0] - total) * (H ** (-0.5)))
-    spread_lanes(bc1, weight * (oq[1] - total) * (H ** (-0.5)))
+    spread_lanes(bc0, weight * (oq[0] * (H ** (-0.5)) - total) * (H ** (-0.5)))
+    spread_lanes(bc1, weight * (oq[1] * (H ** (-0.5)) - total) * (H ** (-0.5)))
 
     h0 = jnp.broadcast_to(onh[0:1, mine], (PAIR, HALF))
     h1 = jnp.broadcast_to(onh[1:2, mine], (PAIR, HALF))
 
     def back(i, adj):
-        for k in range(4):
-            rows = at_t(T - 1 - (i * 4 + k))
-            dh = wide(bc0[rows, :]) * h0 + wide(bc1[rows, :]) * h1
-            adj = dh * vo[rows, :] + adj
+        steps = [at_t(T - 1 - (i * 2 + k)) for k in range(2)]
+        own = [
+            (wide(bc0[rows, :]) * h0 + wide(bc1[rows, :]) * h1) * vo[rows, :] for rows in steps
+        ]
+        for rows, dh in zip(steps, own):
+            adj = dh + adj
             vo[rows, :] = adj
             adj = cc[rows, :] * adj
         return adj
 
-    leaving = lax.fori_loop(0, T // 4, back, jnp.zeros((PAIR, HALF), F32))
+    leaving = lax.fori_loop(0, T // 2, back, jnp.zeros((PAIR, HALF), F32))
     lv[tm] = leaving.astype(BF16)
     prefix_send(5, lv, None, False)
 
@@ -691,33 +710,33 @@
         gx_s[:, cols_of(p)] = gg[p][y, x, z, other_rows, :]
 
     prefix_take(5, lv, None, False)
-    for p in PARTS:
+    for p in RS_PARTS:
         finish(p)
         gradient(p, LINES[0])
         rs_opposite(p, LINES[0])
-    for p in PARTS:
+    for p in RS_PARTS:
         gradient(p, LINES[1])
         rs_opposite(p, LINES[1])
-    for p in PARTS:
+    for p in RS_PARTS:
         rs_neighbours(p, LINES[0])
         gradient(p, LINES[2])
         rs_opposite(p, LINES[2])
-    for p in PARTS:
+    for p in RS_PARTS:
         rs_neighbours(p, LINES[1])
         gradient(p, LINES[3])
         rs_opposite(p, LINES[3])
-    for p in PARTS:
+    for p in RS_PARTS:
         rs_sum(p, LINES[0])
         rs_opposite(p, 4)
-    for p in PARTS:
+    for p in RS_PARTS:
         rs_neighbours(p, LINES[2])
-    for p in PARTS:
+    for p in RS_PARTS:
         rs_sum(p, LINES[1])
         rs_arrived(p, 4)
         rs_neighbour(p, 4, 0)
-    for p in PARTS:
+    for p in RS_PARTS:
         rs_neighbours(p, LINES[3])
-    for p in PARTS:
+    for p in RS_PARTS:
         rs_sum(p, LINES[2])
         rs_neighbour(p, 4, 1)
     prefix_drain(1, ends_t, None, True)
@@ -728,12 +747,13 @@
     prefix_drain(5, lv, None, False)
     remote(wst, wst, d2d_ss.at[0], d2d_rs.at[0], partner).wait_send()
     sums.wait_send()
+    later_q.wait_send()
     for copy in pending:
         copy.wait_send()
     pending.clear()
-    for p in PARTS:
+    for p in RS_PARTS:
         rs_sum(p, LINES[3])
-    for p in PARTS:
+    for p in RS_PARTS:
         rs_sum(p, 4)
         rs_one(p)
     send(gx_s, gx_r, d2d_ss.at[7], d2d_rs.at[7], partner)
@@ -794,17 +814,18 @@
         pltpu.VMEM((TM, 2, PAIR, 128), F32), table, table, ends, ends, ends,
         pltpu.VMEM((PAIR, HALF), F32),
         pltpu.VMEM((2, 2, PAIR, 128), F32), pltpu.VMEM((2, 2, PAIR, 128), F32),
+        pltpu.VMEM((2, 2, PAIR, 128), F32),
         pltpu.VMEM((3, PAIR, 128), F32), pltpu.VMEM((3, PAIR, 128), F32),
         pltpu.VMEM((ROWS, HALF), BF16),
         *[pltpu.VMEM((4, 4, 4, 32, w), F32) for w in WIDTHS],
         *staged, *staged,
         pltpu.VMEM((16, HALF), F32), pltpu.VMEM((16, HALF), F32),
-        pltpu.SemaphoreType.DMA((18,)), pltpu.SemaphoreType.DMA((6 * AG_SEMS + 3,)),
+        pltpu.SemaphoreType.DMA((18,)), pltpu.SemaphoreType.DMA((6 * AG_SEMS + 6,)),
         pltpu.SemaphoreType.DMA((9,)), pltpu.SemaphoreType.DMA((3 * RS_SEMS,)),
         pltpu.SemaphoreType.DMA((6,)), pltpu.SemaphoreType.DMA((6,)),
         pltpu.SemaphoreType.DMA((2,)), pltpu.SemaphoreType.DMA((9,)),
         pltpu.SemaphoreType.DMA((8,)), pltpu.SemaphoreType.DMA((8,)),
-        pltpu.SemaphoreType.DMA((2,)),
+        pltpu.SemaphoreType.DMA((4,)),
     ]
     rows_b, span, width = obs_feats.shape
     grad, returns = pl.pallas_call(

time: 96.9 us -> 94 us (0.970)
  Pallas kernels: 96.1 us -> 93.2 us
    pallas_call x1, Pallas kernels: 94.4 us -> 91.4 us  [shards(): pl.pallas_call(kernel, name='critic_step', out_shape=(jax.ShapeDtypeStruc...]
where the time goes in v5:
time: 94 us; the launch traced here: 93.8 us
  Pallas kernels  93.2 us (99%)
    pallas_call x1, Pallas kernels, shards(): pl.pallas_call(kernel, name='critic_step', out_shape=(jax.ShapeDtypeStruc...  91.4 us

profile of v5, /device:TPU:1, one launch (start us, length us, event | category | flops | bytes accessed | tf_op | source)
XLA Modules:
  0.0 93.8 jit_solution(6356235509830633439)
XLA Ops:
  0.6 91.4 %critic_step.1 = (f32[16,2048]{1,0:T(8,128)}, f32[4,64]{1,0:T(4,128)}) custom-call(bf16[256,2048]{1,0:T(8,128)(2,1)} %bitcast.3, bf16[256,2048]{1,0:T(8,128)(2,1)} %bitcast.4, f32[16,2048]{1,0:T(8,128)} %onw.1, f32[16,2048]{1,0:T(8,128)} %tgw.1, f32[1,2048]{1,0:T(1,128)} %bitcast.5, f32[4,64]{1,0:T(4,128)} %step_in.1, f32[2,2048]{1,0:T(2,128)} %onh_in.1, ...), custom_call_target="tpu_custom_call" | custom-call | tf_op jit(solution)/shard_map/critic_step/pallas_call | solution.py:831
  92.0 1.8 %target_update.1 = (f32[16,2048]{1,0:T(8,128)}, f32[16,2048]{1,0:T(8,128)}, f32[4,64]{1,0:T(4,128)}) custom-call(f32[16,2048]{1,0:T(8,128)} %get-tuple-element.5.grad, f32[4,64]{1,0:T(4,128)} %get-tuple-element.6.returns, f32[16,2048]{1,0:T(8,128)} %onw.1, f32[16,2048]{1,0:T(8,128)} %tgw.1), custom_call_target="tpu_custom_call" | custom-call | tf_op jit(solution)/shard_map/target_update/pallas_call | solution.py:848

commit v6 on v5

--- a/solution.py
+++ b/solution.py
@@ -25,13 +25,14 @@
 VMEM_LIMIT = 56
 SCALE = D ** (-0.5)
 
-WIDTHS_T = (384, 256, 384)
-OFFSETS_T = (0, 384, 640)
+WIDTHS_T = (384, 384, 256)
+OFFSETS_T = (0, 384, 768)
 WIDTHS = (256, 384, 384)
 OFFSETS = (0, 256, 640)
 ORDERS = (("z", "x", "y"), ("y", "z", "x"), ("x", "y", "z"))
 PARTS = (0, 2, 1)
 RS_PARTS = (2, 1, 0)
+PROJECTED = 512
 AG_SEMS = 8
 RS_SEMS = 11
 LINES = (2, 3, 1, 0)
@@ -290,7 +291,7 @@
         qs = [turned(p, axis, d) for d in planes]
 
         def tile(i, _):
-            rows = pl.ds(pl.multiple_of(i * 256, 256), 256)
+            rows = pl.ds(pl.multiple_of(i * PROJECTED, PROJECTED), PROJECTED)
             acc = None if fresh else v[rows, cols]
             for q in qs:
                 where = place(p, FULL, q, FULL) if p == 2 else place(p, FULL, FULL, q)
@@ -305,7 +306,7 @@
             v[rows, cols] = acc
             return 0
 
-        lax.fori_loop(0, ROWS // 256, tile, 0)
+        lax.fori_loop(0, ROWS // PROJECTED, tile, 0)
 
     def scan(m, v, p, ends):
         cols = cols_of(p, m)
@@ -614,17 +615,15 @@
     h1 = jnp.broadcast_to(onh[1:2, mine], (PAIR, HALF))
 
     def back(i, adj):
-        steps = [at_t(T - 1 - (i * 2 + k)) for k in range(2)]
-        own = [
-            (wide(bc0[rows, :]) * h0 + wide(bc1[rows, :]) * h1) * vo[rows, :] for rows in steps
-        ]
-        for rows, dh in zip(steps, own):
-            adj = dh + adj
+        for k in range(4):
+            rows = at_t(T - 1 - (i * 4 + k))
+            dh = wide(bc0[rows, :]) * h0 + wide(bc1[rows, :]) * h1
+            adj = dh * vo[rows, :] + adj
             vo[rows, :] = adj
             adj = cc[rows, :] * adj
         return adj
 
-    leaving = lax.fori_loop(0, T // 2, back, jnp.zeros((PAIR, HALF), F32))
+    leaving = lax.fori_loop(0, T // 4, back, jnp.zeros((PAIR, HALF), F32))
     lv[tm] = leaving.astype(BF16)
     prefix_send(5, lv, None, False)
 
@@ -634,13 +633,13 @@
         both = jnp.concatenate([incoming, incoming], axis=0)
 
         def body(i, _):
-            for k in range(2):
-                rows = pl.ds(pl.multiple_of(i * 32 + k * 16, 16), 16)
+            for k in range(4):
+                rows = pl.ds(pl.multiple_of(i * 64 + k * 16, 16), 16)
                 adj = vo[rows, cols] + tp[rows, cols] * both
                 du[rows, cols] = (ss[rows, cols] * adj).astype(BF16)
             return 0
 
-        lax.fori_loop(0, ROWS // 32, body, 0)
+        lax.fori_loop(0, ROWS // 64, body, 0)
 
     def gradient(p, l):
         where = place(p, FULL, turned(p, 1, l), FULL)

time: 94 us -> 92.8 us (0.987)
  Pallas kernels: 93.2 us -> 92 us
    pallas_call x1, Pallas kernels: 91.4 us -> 90.3 us  [shards(): pl.pallas_call(kernel, name='critic_step', out_shape=(jax.ShapeDtypeStruc...]
where the time goes in v6:
time: 92.8 us; the launch traced here: 92.7 us
  Pallas kernels  92 us (99%)
    pallas_call x1, Pallas kernels, shards(): pl.pallas_call(kernel, name='critic_step', out_shape=(jax.ShapeDtypeStruc...  90.3 us

profile of v6, /device:TPU:1, one launch (start us, length us, event | category | flops | bytes accessed | tf_op | source)
XLA Modules:
  0.0 92.7 jit_solution(3658225911790358223)
XLA Ops:
  0.6 90.3 %critic_step.1 = (f32[16,2048]{1,0:T(8,128)}, f32[4,64]{1,0:T(4,128)}) custom-call(bf16[256,2048]{1,0:T(8,128)(2,1)} %bitcast.3, bf16[256,2048]{1,0:T(8,128)(2,1)} %bitcast.4, f32[16,2048]{1,0:T(8,128)} %onw.1, f32[16,2048]{1,0:T(8,128)} %tgw.1, f32[1,2048]{1,0:T(1,128)} %bitcast.5, f32[4,64]{1,0:T(4,128)} %step_in.1, f32[2,2048]{1,0:T(2,128)} %onh_in.1, ...), custom_call_target="tpu_custom_call" | custom-call | tf_op jit(solution)/shard_map/critic_step/pallas_call | solution.py:830
  90.9 1.8 %target_update.1 = (f32[16,2048]{1,0:T(8,128)}, f32[16,2048]{1,0:T(8,128)}, f32[4,64]{1,0:T(4,128)}) custom-call(f32[16,2048]{1,0:T(8,128)} %get-tuple-element.5.grad, f32[4,64]{1,0:T(4,128)} %get-tuple-element.6.returns, f32[16,2048]{1,0:T(8,128)} %onw.1, f32[16,2048]{1,0:T(8,128)} %tgw.1), custom_call_target="tpu_custom_call" | custom-call | tf_op jit(solution)/shard_map/target_update/pallas_call | solution.py:847

commit v7 on v6

--- a/solution.py
+++ b/solution.py
@@ -25,13 +25,13 @@
 VMEM_LIMIT = 56
 SCALE = D ** (-0.5)
 
-WIDTHS_T = (384, 384, 256)
-OFFSETS_T = (0, 384, 768)
-WIDTHS = (256, 384, 384)
-OFFSETS = (0, 256, 640)
+WIDTHS_T = (256, 384, 384)
+OFFSETS_T = (0, 256, 640)
+WIDTHS = (384, 256, 384)
+OFFSETS = (0, 384, 640)
 ORDERS = (("z", "x", "y"), ("y", "z", "x"), ("x", "y", "z"))
-PARTS = (0, 2, 1)
-RS_PARTS = (2, 1, 0)
+PARTS = (1, 0, 2)
+RS_PARTS = (2, 0, 1)
 PROJECTED = 512
 AG_SEMS = 8
 RS_SEMS = 11
@@ -549,18 +549,11 @@
     for l in (0, 3, 1):
         ag_line_last(1, l)
     project_planes(1, 2, (0, 1, 3), True)
-    ag_three_last(1, 0)
-    project_planes(1, 0, (2,), False)
-    scan(1, vo, PARTS[0], ends_o)
-    prefix_send(2 + PARTS[0], ends_o, PARTS[0], True)
-    ag_line_last(1, 2)
-    project_planes(1, 2, (2,), False)
-    scan(1, vo, PARTS[1], ends_o)
-    prefix_send(2 + PARTS[1], ends_o, PARTS[1], True)
-    ag_three_last(1, 1)
-    project_planes(1, 1, (2,), False)
-    scan(1, vo, PARTS[2], ends_o)
-    prefix_send(2 + PARTS[2], ends_o, PARTS[2], True)
+    for p in PARTS:
+        ag_line_last(1, 2) if p == 2 else ag_three_last(1, p)
+        project_planes(1, p, (2,), False)
+        scan(1, vo, p, ends_o)
+        prefix_send(2 + p, ends_o, p, True)
     prefix_take(1, ends_t, None, True)
     for p in PARTS:
         quality(0, vt, tgh, p, p == PARTS[0], False)

time: 92.8 us -> 91.4 us (0.985)
  Pallas kernels: 92 us -> 90.6 us
    pallas_call x1, Pallas kernels: 90.3 us -> 88.8 us  [shards(): pl.pallas_call(kernel, name='critic_step', out_shape=(jax.ShapeDtypeStruc...]
where the time goes in v7:
time: 91.4 us; the launch traced here: 91.3 us
  Pallas kernels  90.6 us (99%)
    pallas_call x1, Pallas kernels, shards(): pl.pallas_call(kernel, name='critic_step', out_shape=(jax.ShapeDtypeStruc...  88.8 us

profile of v7, /device:TPU:1, one launch (start us, length us, event | category | flops | bytes accessed | tf_op | source)
XLA Modules:
  0.0 91.3 jit_solution(3849302267133560895)
XLA Ops:
  0.6 88.8 %critic_step.1 = (f32[16,2048]{1,0:T(8,128)}, f32[4,64]{1,0:T(4,128)}) custom-call(bf16[256,2048]{1,0:T(8,128)(2,1)} %bitcast.3, bf16[256,2048]{1,0:T(8,128)(2,1)} %bitcast.4, f32[16,2048]{1,0:T(8,128)} %onw.1, f32[16,2048]{1,0:T(8,128)} %tgw.1, f32[1,2048]{1,0:T(1,128)} %bitcast.5, f32[4,64]{1,0:T(4,128)} %step_in.1, f32[2,2048]{1,0:T(2,128)} %onh_in.1, ...), custom_call_target="tpu_custom_call" | custom-call | tf_op jit(solution)/shard_map/critic_step/pallas_call | solution.py:823
  89.5 1.8 %target_update.1 = (f32[16,2048]{1,0:T(8,128)}, f32[16,2048]{1,0:T(8,128)}, f32[4,64]{1,0:T(4,128)}) custom-call(f32[16,2048]{1,0:T(8,128)} %get-tuple-element.5.grad, f32[4,64]{1,0:T(4,128)} %get-tuple-element.6.returns, f32[16,2048]{1,0:T(8,128)} %onw.1, f32[16,2048]{1,0:T(8,128)} %tgw.1), custom_call_target="tpu_custom_call" | custom-call | tf_op jit(solution)/shard_map/target_update/pallas_call | solution.py:840

commit v8 on v7

--- a/solution.py
+++ b/solution.py
@@ -546,11 +546,14 @@
         ag_three_forward(1, p, 2)
     for p in (0, 1):
         project_planes(1, p, (1, 3), False)
-    for l in (0, 3, 1):
-        ag_line_last(1, l)
-    project_planes(1, 2, (0, 1, 3), True)
     for p in PARTS:
-        ag_line_last(1, 2) if p == 2 else ag_three_last(1, p)
+        if p == 2:
+            for l in (0, 3, 1):
+                ag_line_last(1, l)
+            project_planes(1, p, (0, 1, 3), True)
+            ag_line_last(1, 2)
+        else:
+            ag_three_last(1, p)
         project_planes(1, p, (2,), False)
         scan(1, vo, p, ends_o)
         prefix_send(2 + p, ends_o, p, True)

time: 91.4 us -> 91.3 us (level)
  no operation moved by 1% of the time
where the time goes in v8:
time: 91.3 us; the launch traced here: 91.2 us
  Pallas kernels  90.5 us (99%)
    pallas_call x1, Pallas kernels, shards(): pl.pallas_call(kernel, name='critic_step', out_shape=(jax.ShapeDtypeStruc...  88.7 us

profile of v8, /device:TPU:1, one launch (start us, length us, event | category | flops | bytes accessed | tf_op | source)
XLA Modules:
  0.0 91.2 jit_solution(1926256513199684806)
XLA Ops:
  0.6 88.7 %critic_step.1 = (f32[16,2048]{1,0:T(8,128)}, f32[4,64]{1,0:T(4,128)}) custom-call(bf16[256,2048]{1,0:T(8,128)(2,1)} %bitcast.3, bf16[256,2048]{1,0:T(8,128)(2,1)} %bitcast.4, f32[16,2048]{1,0:T(8,128)} %onw.1, f32[16,2048]{1,0:T(8,128)} %tgw.1, f32[1,2048]{1,0:T(1,128)} %bitcast.5, f32[4,64]{1,0:T(4,128)} %step_in.1, f32[2,2048]{1,0:T(2,128)} %onh_in.1, ...), custom_call_target="tpu_custom_call" | custom-call | tf_op jit(solution)/shard_map/critic_step/pallas_call | solution.py:826
  89.4 1.8 %target_update.1 = (f32[16,2048]{1,0:T(8,128)}, f32[16,2048]{1,0:T(8,128)}, f32[4,64]{1,0:T(4,128)}) custom-call(f32[16,2048]{1,0:T(8,128)} %get-tuple-element.5.grad, f32[4,64]{1,0:T(4,128)} %get-tuple-element.6.returns, f32[16,2048]{1,0:T(8,128)} %onw.1, f32[16,2048]{1,0:T(8,128)} %tgw.1), custom_call_target="tpu_custom_call" | custom-call | tf_op jit(solution)/shard_map/target_update/pallas_call | solution.py:843
